TPU v7x, 32 devices: a whole 2x2x4 slice. The times are simulated.
32 devices in a mesh: site: 2 (over y), rows: 8 (over z, core), width: 2 (over x).
Axes of the slice: x: 2, y: 2, z: 4, core: 2. Of those that a mesh axis runs over, the one named last changes fastest.
Arguments:
- one_query: float32 [14336, 7168], P(('site', 'rows'), 'width'), parts along dimension 0, may hold values from -0.09375 to 0.09375
- other_query: float32 [14336, 7168], P(('site', 'rows'), 'width'), parts along dimension 0, may hold values from -0.0625 to 0.0625
- one_key: float32 [14336, 1024], P(('site', 'rows'), 'width'), parts along dimension 0, may hold values from -0.09375 to 0.09375
- other_key: float32 [14336, 1024], P(('site', 'rows'), 'width'), parts along dimension 0, may hold values from -0.0625 to 0.0625
- one_value: float32 [14336, 1024], P(('site', 'rows'), 'width'), parts along dimension 0, may hold values from -0.09375 to 0.09375
- other_value: float32 [14336, 1024], P(('site', 'rows'), 'width'), parts along dimension 0, may hold values from -0.0625 to 0.0625
- mix_share: float32 [14336], P(('site', 'rows')), parts along dimension 0, may hold values from 0.2 to 0.8
- norm_train: float32 [14336], P(('site', 'rows', 'width')), parts along dimension 0, may hold values from 0.25 to 1.75
- norm_step: float32 [14336], P(('site', 'rows', 'width')), parts along dimension 0, may hold values from -0.3 to 0.3
Outputs:
- serving_query: bfloat16 [14336, 7168], P('site', 'width'), parts along dimension 0
- serving_key: bfloat16 [14336, 1024], P('site', 'width'), parts along dimension 0
- serving_value: bfloat16 [14336, 1024], P('site', 'width'), parts along dimension 0
- scale_query: float32 [14336], P(('site', 'width')), parts along dimension 0
- scale_key: float32 [2048], P(('site', 'width')), parts along dimension 0
- scale_value: float32 [2048], P(('site', 'width')), parts along dimension 0
- serve_norm: bfloat16 [14336], P('site'), parts along dimension 0
There are 2 independent parts, one for each index of `site`. A program takes and returns all parts, laid end to end along the dimension named above; each array names one. Nothing has to cross between parts.
All inputs are finite; a program needn't handle non-finite values. Where the computation divides by a largest or mean magnitude, that divisor is 1e-20 or more.
Results may differ from a plain program's by a relative error of at most 0.001.
Values may be sent and summed in bfloat16 or wider, within the bound.
A program may use at most 256 MiB of HBM per device.

v0:
```python
import functools

import jax
import jax.numpy as jnp
from jax import lax
from jax.experimental import pallas as pl
from jax.experimental.pallas import tpu as pltpu
from jax.sharding import PartitionSpec as P


MESH = pl.DeviceIdType.MESH
CORES = 2
LANES = 128
LATE = 2
AHEAD = 3


def merge(
    ranks,
    widths,
    one_query,
    other_query,
    one_key,
    other_key,
    one_value,
    other_value,
    mix_row,
    norm_train,
    norm_step,
    query,
    key,
    value,
    far_query,
    far_key,
    far_value,
    scale_query,
    scale_key,
    scale_value,
    norms,
    one,
    other,
    narrow,
    mix,
    peaks,
    load_sem,
    out_sem,
    far_sem,
    peak_send,
    peak_recv,
    norm_send,
    norm_recv,
    up_send,
    up_recv,
    down_send,
    down_recv,
    side_send,
    side_recv,
):
    depth, span = one_key.shape
    parts = one_query.shape[1] // span
    early = parts - LATE
    chips = ranks // CORES
    me = lax.axis_index("rows")
    across = lax.axis_index("width")
    chip, core = me // CORES, me % CORES
    partner = chip * CORES + 1 - core
    group = ranks * widths
    block = 32 if depth % 32 == 0 else depth
    late_parts = range(early, parts + 2)

    def is_static(k):
        return isinstance(k, int)

    def loads(k):
        if is_static(k) and k >= parts:
            sources = (one_key, other_key) if k == parts else (one_value, other_value)
        else:
            cut = pl.ds(pl.multiple_of(k * span, span), span)
            sources = one_query.at[:, cut], other_query.at[:, cut]
        return [
            pltpu.make_async_copy(source, target.at[k], load_sem.at[i, k])
            for i, (source, target) in enumerate(zip(sources, (one, other)))
        ]

    def load(k):
        for copy in loads(k):
            copy.start()

    pl.loop(0, AHEAD)(load)

    barrier = pltpu.get_barrier_semaphore()
    mine = me * widths + across

    @pl.loop(1, group)
    def _(step):
        to = lax.rem(mine + step, group)
        pl.semaphore_signal(
            barrier,
            inc=1,
            device_id={"rows": to // widths, "width": lax.rem(to, widths)},
            device_id_type=MESH,
        )

    norms[mine] = norm_train[...] + norm_step[...]

    for first in range(0, mix.shape[0], LANES):
        row = mix_row[:, first : first + LANES]
        mix[first : first + LANES] = jnp.broadcast_to(row, (LANES, LANES)).T

    def send_peaks(k):
        @pl.loop(1, ranks)
        def _(step):
            pltpu.make_async_remote_copy(
                src_ref=peaks.at[k, me],
                dst_ref=peaks.at[k, me],
                send_sem=peak_send.at[k],
                recv_sem=peak_recv.at[k],
                device_id={"rows": lax.rem(me + step, ranks)},
                device_id_type=MESH,
            ).start()

    def mixed(k):
        for copy in loads(k):
            copy.wait()
        if is_static(k):
            if k + AHEAD < parts + 2:
                load(k + AHEAD)
        else:

            @pl.when(k + AHEAD < parts)
            def _():
                load(k + AHEAD)

            for tail in (parts, parts + 1):

                @pl.when(k + AHEAD == tail)
                def _():
                    load(tail)

        def step(b, top):
            rows = pl.ds(pl.multiple_of(b * block, block), block)
            share = jnp.concatenate([mix[rows]] * (span // LANES), axis=1)
            whole = share * one[k, rows] + (1.0 - share) * other[k, rows]
            one[k, rows] = whole
            return jnp.maximum(top, jnp.max(jnp.abs(whole).reshape(-1, 8, span), axis=0))

        top = lax.fori_loop(0, depth // block, step, jnp.zeros((8, span), jnp.float32))
        peaks[k, me] = jnp.max(top, axis=0, keepdims=True)

    def is_tail(k):
        return is_static(k) and k >= parts

    def hops(k):
        return chips - 2 if is_static(k) and k >= early else chips - 1

    def slot(k, rank):
        rows = pl.ds(pl.multiple_of(rank * depth, depth), depth)
        if is_tail(k):
            return (key if k == parts else value).at[rows]
        return query.at[rows, pl.ds(pl.multiple_of(k * span, span), span)]

    def send(k, rank, to, send_sem, recv_sem, source=None):
        return pltpu.make_async_remote_copy(
            src_ref=slot(k, rank) if source is None else source,
            dst_ref=slot(k, rank),
            send_sem=send_sem,
            recv_sem=recv_sem,
            device_id={"rows": to},
            device_id_type=MESH,
        )

    def go_up(k, hop, source=None):
        return send(k, me - CORES * hop, me + CORES, up_send.at[hop, k], up_recv.at[hop, k], source)

    def go_down(k, hop, source=None):
        return send(
            k, me + CORES * hop, me - CORES, down_send.at[hop, k], down_recv.at[hop, k], source
        )

    def go_side(k, hop, source=None):
        index = hop + chips - 1
        return send(
            k, me + CORES * hop, partner, side_send.at[index, k], side_recv.at[index, k], source
        )

    def from_side(k, hop):
        index = hop + chips - 1
        return send(
            k, partner + CORES * hop, partner, side_send.at[index, k], side_recv.at[index, k]
        )

    def from_below(k, hop):
        return send(k, me - CORES * (hop + 1), me - CORES, up_send.at[hop, k], up_recv.at[hop, k])

    def from_above(k, hop):
        return send(
            k, me + CORES * (hop + 1), me + CORES, down_send.at[hop, k], down_recv.at[hop, k]
        )

    has_below, has_above = chip >= 1, chip < chips - 1

    def keep(k):
        return pltpu.make_async_copy(narrow.at[k], slot(k, me), out_sem.at[k])

    def scaled(k, scale_ref, cut):
        everyone = peaks.at[k, pl.ds(0, ranks - 1)]
        pltpu.make_async_copy(everyone, everyone, peak_recv.at[k]).wait()
        scale = jnp.max(peaks[k], axis=0)
        scale_ref[:, cut] = scale

        @pl.loop(0, depth // block)
        def _(b):
            rows = pl.ds(pl.multiple_of(b * block, block), block)
            narrow[k, rows] = (one[k, rows] / scale).astype(jnp.bfloat16)

        source = narrow.at[k]

        @pl.when(has_below)
        def _():
            go_down(k, 0, source).start()

        @pl.when(has_above)
        def _():
            go_up(k, 0, source).start()

        go_side(k, 0, source).start()
        keep(k).start()

    def part_cut(k):
        return pl.ds(pl.multiple_of(k * span, span), span)

    mixed(0)
    pl.semaphore_wait(barrier, group - 1)
    send_peaks(0)

    def advance(k):
        mixed(k)
        send_peaks(k)

    lag = min(2, parts)
    pl.loop(1, lag)(advance)

    @pl.loop(0, parts - lag)
    def _(k):
        advance(k + lag)
        scaled(k, scale_query, part_cut(k))

    advance(parts)
    advance(parts + 1)

    @pl.loop(1, group)
    def _(step):
        to = lax.rem(mine + step, group)
        pltpu.make_async_remote_copy(
            src_ref=norms.at[mine],
            dst_ref=norms.at[mine],
            send_sem=norm_send,
            recv_sem=norm_recv,
            device_id={"rows": to // widths, "width": lax.rem(to, widths)},
            device_id_type=MESH,
        ).start()

    @pl.loop(parts - lag, parts)
    def _(k):
        scaled(k, scale_query, part_cut(k))

    scaled(parts, scale_key, slice(None))
    scaled(parts + 1, scale_value, slice(None))

    def far_copy(k, rank):
        if is_tail(k):
            target = far_key if k == parts else far_value
        else:
            target = far_query.at[:, pl.ds((k - early) * span, span)]
        return pltpu.make_async_copy(slot(k, rank), target, far_sem.at[k - early])

    def relay(k, hop):
        onward = hop < hops(k)
        is_far = is_static(k) and k >= early

        @pl.when(chip >= hop)
        def _():
            from_below(k, hop - 1).wait_recv()

            @pl.when(has_above & onward)
            def _():
                go_up(k, hop).start()

            go_side(k, -hop).start()

            if is_far:

                @pl.when((hop == chips - 2) & (chip == chips - 2))
                def _():
                    far_copy(k, me - CORES * hop).start()

        @pl.when(chip + hop < chips)
        def _():
            from_above(k, hop - 1).wait_recv()

            @pl.when(has_below & onward)
            def _():
                go_down(k, hop).start()

            go_side(k, hop).start()

            if is_far:

                @pl.when((hop == chips - 2) & (chip == 1))
                def _():
                    far_copy(k, me + CORES * hop).start()

    @pl.loop(1, chips - 1)
    def _(hop):
        pl.loop(0, early)(lambda k: relay(k, hop))
        for k in late_parts:
            relay(k, hop)

    pl.loop(0, early)(lambda k: relay(k, chips - 1))

    def finish(k):
        keep(k).wait()

        @pl.loop(0, hops(k))
        def _(hop):
            @pl.when((chip >= hop) & has_above)
            def _():
                go_up(k, hop).wait_send()

            @pl.when((chip + hop < chips) & has_below)
            def _():
                go_down(k, hop).wait_send()

        @pl.loop(0, chips)
        def _(origin):
            @pl.when((origin - chip <= hops(k)) & (chip - origin <= hops(k)))
            def _():
                go_side(k, origin - chip).wait_send()
                from_side(k, origin - chip).wait_recv()

        if is_static(k):

            @pl.when((chip == 1) | (chip == chips - 2))
            def _():
                far_copy(k, me).wait()

    for k in late_parts:
        finish(k)

    def settle(k):
        everyone = peaks.at[k, pl.ds(0, ranks - 1)]
        pltpu.make_async_copy(everyone, everyone, peak_send.at[k]).wait()

    pl.loop(0, parts + 2)(settle)
    others = norms.at[pl.ds(0, group - 1)]
    pltpu.make_async_copy(others, others, norm_recv).wait()
    pltpu.make_async_copy(others, others, norm_send).wait()
    pl.loop(0, early)(finish)


def stream(total, incoming, outgoing, ring):
    ahead = ring // 2

    def head():
        for i in range(min(ahead, total)):
            incoming(i, True)

    def body():
        @pl.loop(0, total)
        def _(i):
            incoming(i, False)
            outgoing(i).start()

            @pl.when(i + ahead < total)
            def _():
                @pl.when(i + ahead >= ring)
                def _():
                    outgoing(i + ahead - ring).wait()

                incoming(i + ahead, True)

    def drain():
        @pl.loop(max(0, total - ring), total)
        def _(i):
            outgoing(i).wait()

    return head, body, drain


def act(copy, begin):
    if begin:
        copy.start()
    else:
        copy.wait()


def settle_kernel(query, value, new_query, new_value, done, wide_buf, slim_buf, sems):
    ring = wide_buf.shape[0]

    def plan(source, target, buf, at):
        step = buf.shape[1]
        cols = pl.ds(0, buf.shape[2])

        def rows(i):
            return pl.ds(pl.multiple_of(i * step, step), step)

        def incoming(i, begin):
            place = lax.rem(i, ring)
            act(
                pltpu.make_async_copy(
                    source.at[rows(i), cols], buf.at[place], sems.at[at, place]
                ),
                begin,
            )

        def outgoing(i):
            place = lax.rem(i, ring)
            return pltpu.make_async_copy(
                buf.at[place], target.at[rows(i), cols], sems.at[at + 1, place]
            )

        return stream(source.shape[0] // step, incoming, outgoing, ring)

    first = plan(query, new_query, wide_buf, 0)
    second = plan(value, new_value, slim_buf, 2)
    first[0]()
    first[1]()
    second[0]()
    second[1]()
    first[2]()
    second[2]()
    done[...] = jnp.zeros_like(done)


def chunk_of(rows, most):
    step = rows
    while step > most and step % 32 == 0:
        step //= 2
    return step


def settled(query, value, wide, ring=8):
    rows, span = value.shape
    step = chunk_of(rows, 128)
    slim = chunk_of(rows, 512)
    anywhere = pl.BlockSpec(memory_space=pl.ANY)
    moved = 4 * rows * (wide + span)
    return pl.pallas_call(
        settle_kernel,
        out_shape=(
            jax.ShapeDtypeStruct(query.shape, query.dtype),
            jax.ShapeDtypeStruct(value.shape, value.dtype),
            jax.ShapeDtypeStruct((8, LANES), jnp.float32),
        ),
        in_specs=[anywhere] * 2,
        out_specs=(anywhere, anywhere, pl.BlockSpec(memory_space=pltpu.VMEM)),
        scratch_shapes=[
            pltpu.VMEM((ring, step, wide), query.dtype),
            pltpu.VMEM((ring, slim, span), value.dtype),
            pltpu.SemaphoreType.DMA((4, ring)),
        ],
        compiler_params=pltpu.CompilerParams(vmem_limit_bytes=60 * 2**20),
        cost_estimate=pl.CostEstimate(
            flops=0, bytes_accessed=moved, transcendentals=0
        ),
    )(query, value)


def far_ranks(ranks):
    chips = ranks // CORES
    me = lax.axis_index("rows")
    chip, core = me // CORES, me % CORES
    at_end = (chip == 0) | (chip == chips - 1)
    away = jnp.where(chip == 0, chips - 1, 0) * CORES
    return at_end, away + core, away + 1 - core


def blend_kernel(
    ranks, wide, _, query, key, got_query, side_query, got_key, side_key, done,
    new_query, new_key, query_buf, key_buf, sems,
):
    depth = got_key.shape[0]
    at_end, straight, crossed = far_ranks(ranks)
    ring = query_buf.shape[0]
    late = query_buf.shape[2]

    def plan(source, got, side, target, buf, cols, at):
        def rows(i):
            return pl.ds(pl.multiple_of(i * depth, depth), depth)

        def incoming(i, begin):
            place = lax.rem(i, ring)

            def copy(origin):
                act(pltpu.make_async_copy(origin, buf.at[place], sems.at[at, place]), begin)

            if not begin:
                copy(source.at[rows(i), cols])
                return
            is_got = at_end & (i == straight)
            is_side = at_end & (i == crossed)
            pl.when(is_got)(lambda: copy(got))
            pl.when(is_side)(lambda: copy(side))
            pl.when(jnp.logical_not(is_got | is_side))(lambda: copy(source.at[rows(i), cols]))

        def outgoing(i):
            place = lax.rem(i, ring)
            return pltpu.make_async_copy(
                buf.at[place], target.at[rows(i), cols], sems.at[at + 1, place]
            )

        return stream(ranks, incoming, outgoing, ring)

    first = plan(
        query, got_query, side_query, new_query, query_buf, pl.ds(wide, late), 0
    )
    second = plan(key, got_key, side_key, new_key, key_buf, pl.ds(0, key_buf.shape[2]), 2)
    first[0]()
    second[0]()
    first[1]()
    second[1]()
    first[2]()
    second[2]()


def blended(
    ranks, wide, new_query, query, key, got_query, side_query, got_key, side_key, done, ring=4
):
    depth, span = got_key.shape
    late = got_query.shape[1]
    anywhere = pl.BlockSpec(memory_space=pl.ANY)
    moved = 4 * ranks * depth * (late + span)
    return pl.pallas_call(
        functools.partial(blend_kernel, ranks, wide),
        out_shape=(
            jax.ShapeDtypeStruct(query.shape, query.dtype),
            jax.ShapeDtypeStruct(key.shape, key.dtype),
        ),
        in_specs=[anywhere] * 8,
        out_specs=(anywhere, anywhere),
        scratch_shapes=[
            pltpu.VMEM((ring, depth, late), query.dtype),
            pltpu.VMEM((ring, depth, span), key.dtype),
            pltpu.SemaphoreType.DMA((4, ring)),
        ],
        input_output_aliases={0: 0},
        compiler_params=pltpu.CompilerParams(vmem_limit_bytes=60 * 2**20),
        cost_estimate=pl.CostEstimate(
            flops=0, bytes_accessed=moved, transcendentals=0
        ),
    )(new_query, query, key, got_query, side_query, got_key, side_key, done)


def place_kernel(ranks, _, got, side, target, buf, sems):
    at_end, straight, crossed = far_ranks(ranks)
    depth = got.shape[0]
    step = buf.shape[1]
    cuts = depth // step

    @pl.when(at_end)
    def _():
        def incoming(i):
            source = (got, side)[i // cuts]
            rows = pl.ds(i % cuts * step, step)
            return pltpu.make_async_copy(source.at[rows], buf.at[i], sems.at[0, i])

        def outgoing(i):
            rank = (straight, crossed)[i // cuts]
            rows = pl.ds(pl.multiple_of(rank * depth + i % cuts * step, step), step)
            return pltpu.make_async_copy(buf.at[i], target.at[rows], sems.at[1, i])

        for i in range(2 * cuts):
            incoming(i).start()
        for i in range(2 * cuts):
            incoming(i).wait()
            outgoing(i).start()
        for i in range(2 * cuts):
            outgoing(i).wait()


def placed(ranks, whole, got, side, cuts=4):
    depth, span = got.shape
    anywhere = pl.BlockSpec(memory_space=pl.ANY)
    return pl.pallas_call(
        functools.partial(place_kernel, ranks),
        out_shape=jax.ShapeDtypeStruct(whole.shape, whole.dtype),
        in_specs=[anywhere] * 3,
        out_specs=anywhere,
        scratch_shapes=[
            pltpu.VMEM((2 * cuts, depth // cuts, span), whole.dtype),
            pltpu.SemaphoreType.DMA((2, 2 * cuts)),
        ],
        input_output_aliases={0: 0},
        compiler_params=pltpu.CompilerParams(vmem_limit_bytes=8 * 2**20),
        cost_estimate=pl.CostEstimate(
            flops=0, bytes_accessed=8 * depth * span, transcendentals=0
        ),
    )(whole, got, side)


def shards(
    ranks,
    widths,
    one_query,
    other_query,
    one_key,
    other_key,
    one_value,
    other_value,
    mix_share,
    norm_train,
    norm_step,
):
    depth, span = one_key.shape
    wide = one_query.shape[1]
    parts = wide // span
    chips = ranks // CORES
    group = ranks * widths
    bit = norm_train.shape[0]
    late = LATE * span
    tall = -(-depth // LANES) * LANES
    mix_row = mix_share[None]
    if tall != depth:
        mix_row = jnp.pad(mix_row, ((0, 0), (0, tall - depth)))
    shape = jax.ShapeDtypeStruct
    anywhere = pl.BlockSpec(memory_space=pl.ANY)
    near = pl.BlockSpec(memory_space=pltpu.VMEM)
    dma = pltpu.SemaphoreType.DMA
    (
        query, key, value, far_query, far_key, far_value,
        scale_query, scale_key, scale_value, norms,
    ) = pl.pallas_call(
        functools.partial(merge, ranks, widths),
        out_shape=(
            shape((ranks * depth, wide), jnp.bfloat16),
            shape((ranks * depth, span), jnp.bfloat16),
            shape((ranks * depth, span), jnp.bfloat16),
            shape((depth, late), jnp.bfloat16),
            shape((depth, span), jnp.bfloat16),
            shape((depth, span), jnp.bfloat16),
            shape((1, wide), jnp.float32),
            shape((1, span), jnp.float32),
            shape((1, span), jnp.float32),
            shape((group, 1, bit), jnp.float32),
        ),
        in_specs=[anywhere] * 6 + [near] * 3,
        out_specs=[anywhere] * 6 + [near] * 4,
        scratch_shapes=[
            pltpu.VMEM((parts + 2, depth, span), jnp.float32),
            pltpu.VMEM((parts + 2, depth, span), jnp.float32),
            pltpu.VMEM((parts + 2, depth, span), jnp.bfloat16),
            pltpu.VMEM((tall, LANES), jnp.float32),
            pltpu.VMEM((parts + 2, ranks, 1, span), jnp.float32),
            dma((2, parts + 2)),
            dma((parts + 2,)),
            dma((LATE + 2,)),
            dma((parts + 2,)),
            dma((parts + 2,)),
            dma,
            dma,
            dma((chips - 1, parts + 2)),
            dma((chips - 1, parts + 2)),
            dma((chips - 1, parts + 2)),
            dma((chips - 1, parts + 2)),
            dma((2 * chips - 1, parts + 2)),
            dma((2 * chips - 1, parts + 2)),
        ],
        compiler_params=pltpu.CompilerParams(
            collective_id=0, has_side_effects=True, vmem_limit_bytes=56 * 2**20
        ),
    )(
        one_query,
        other_query,
        one_key,
        other_key,
        one_value,
        other_value,
        mix_row,
        norm_train[None],
        norm_step[None],
    )
    ends = (0, chips - 1)
    out = [
        (near * CORES + c, end * CORES + c)
        for near, end in ((1, 0), (chips - 2, chips - 1))
        for c in range(CORES)
    ]
    across = [(end * CORES + c, end * CORES + 1 - c) for end in ends for c in range(CORES)]

    def last_hop(piece):
        return lax.ppermute(piece, "rows", out)

    def to_side(piece):
        return lax.ppermute(piece, "rows", across)

    got_query = last_hop(far_query)
    got_key = last_hop(far_key)
    got_value = last_hop(far_value)
    new_query, new_value, done = settled(query, value, wide - late)
    small = (
        scale_query[0],
        scale_key[0],
        scale_value[0],
        norms.reshape(-1).astype(jnp.bfloat16),
    )
    got_query, got_key, done = lax.optimization_barrier((got_query, got_key, done))
    side_query, side_key = to_side(got_query), to_side(got_key)
    new_query, new_key = blended(
        ranks, wide - late, new_query, query, key, got_query, side_query, got_key, side_key, done
    )
    got_value, new_query, new_key, small = lax.optimization_barrier(
        (got_value, new_query, new_key, small)
    )
    new_value = placed(ranks, new_value, got_value, to_side(got_value))
    return (new_query, new_key, new_value, *small)


def solution(mesh):
    in_specs = (
        P(("site", "rows"), "width"),
        P(("site", "rows"), "width"),
        P(("site", "rows"), "width"),
        P(("site", "rows"), "width"),
        P(("site", "rows"), "width"),
        P(("site", "rows"), "width"),
        P(("site", "rows")),
        P(("site", "rows", "width")),
        P(("site", "rows", "width")),
    )
    out_specs = (
        P("site", "width"),
        P("site", "width"),
        P("site", "width"),
        P(("site", "width")),
        P(("site", "width")),
        P(("site", "width")),
        P("site"),
    )
    body = functools.partial(shards, mesh.shape["rows"], mesh.shape["width"])

    return jax.shard_map(body, mesh=mesh, in_specs=in_specs, out_specs=out_specs, check_vma=False)
```

profile of v0, /device:TPU:0, one launch (start us, length us, event | category | flops | bytes accessed | tf_op | source)
XLA Modules:
  0.0 575.9 jit_solution(13778815230066348812)
XLA Ops:
  0.6 1.3 broadcast_in_dim.9.mix_row
  1.9 471.9 %shard_map.144 = (bf16[7168,3584]{1,0:T(8,128)(2,1)}, bf16[7168,512]{1,0:T(8,128)(2,1)}, bf16[7168,512]{1,0:T(8,128)(2,1)}, bf16[896,1024]{1,0:T(8,128)(2,1)}, b...) custom-call(f32[896,3584]{1,0:T(8,128)} %one_query.1, ...), custom_call_target="tpu_custom_call" | custom-call | tf_op jit(solution)/shard_map/pallas_call | solution.py:632
  473.8 1.3 collective-permute-start.1
  475.1 1.3 collective-permute-start.2
  476.4 0.0 copy-start.1
  476.4 0.0 copy-start.2
  476.4 33.8 %shard_map.145 = (bf16[7168,3584]{1,0:T(8,128)(2,1)}, bf16[7168,512]{1,0:T(8,128)(2,1)}, f32[8,128]{1,0:T(8,128)}) custom-call(bf16[7168,3584]{1,0:T(8,128)(2,1)} %get-tuple-element.33.query, bf16[7168,512]{1,0:T(8,128)(2,1)} %get-tuple-element.34.value), custom_call_target="tpu_custom_call" | custom-call | bytes 88080384 | tf_op jit(solution)/shard_map/pallas_call | solution.py:448
  510.2 27.8 %collective-permute-done.2.got_key = bf16[896,512]{1,0:T(8,128)(2,1)} collective-permute-done((bf16[896,512]{1,0:T(8,128)(2,1)}, bf16[896,512]{1,0:T(8,128)(2,1)}, u32[]{:S(2)}, u32[]{:S(2)}) %collective-permute-start.2) | collective-permute-done | bytes 917536 | tf_op jit(solution)/shard_map/ppermute | solution.py:691
  537.9 0.0 collective-permute-done.1.got_query
  537.9 0.0 copy-start
  537.9 1.9 collective-permute-start.3
  539.9 2.4 collective-permute-start.4
  542.3 1.3 collective-permute-start
  543.6 0.0 copy-done.1
  543.6 0.1 convert_reduce_fusion
  543.7 0.7 convert_element_type.7
  544.4 0.0 copy-done.2
  544.4 0.6 reduce
  545.0 0.0 collective-permute-done.4.side_key
  545.1 0.0 collective-permute-done.3.side_query
  545.1 0.0 copy-done
  545.1 18.1 %shard_map.146 = (bf16[7168,3584]{1,0:T(8,128)(2,1)}, bf16[7168,512]{1,0:T(8,128)(2,1)}) custom-call(bf16[7168,3584]{1,0:T(8,128)(2,1)} %get-tuple-element.35._, bf16[7168,3584]{1,0:T(8,128)(2,1)} %get-tuple-element.33.query, bf16[7168,512]{1,0:T(8,128)(2,1)} %get-tuple-element.36.key, bf16[896,1024]{1,0:T(8,128)(2,1)} %copy-done, ...), custom_call_target="tpu_custom_call", output_to_operand_aliasing={{0}: (0, {})} | custom-call | bytes 44040192 | tf_op jit(solution)/shard_map/pallas_call | solution.py:533
  563.1 3.5 collective-permute-done.got
  566.7 1.9 collective-permute-start.5
  568.6 2.4 collective-permute-done.5.side
  571.0 0.0 copy-start.4
  571.0 0.0 copy-start.3
  571.0 3.7 shard_map.147
  574.7 0.0 copy-done.4
  574.7 0.6 copy.22
  575.3 0.0 copy-done.3
  575.3 0.6 copy.23
Async XLA Ops:
  473.8 64.2 %collective-permute-start.1 = (bf16[896,1024]{1,0:T(8,128)(2,1)}, bf16[896,1024]{1,0:T(8,128)(2,1)S(1)}, u32[]{:S(2)}, u32[]{:S(2)}) collective-permute-start(bf16[896,1024]{1,0:T(8,128)(2,1)} %get-tuple-element.37), channel_id=1, source_target_pairs={{4,0},{6,2},{8,12},{10,14},{5,1},{7,3},{9,13},{11,15},{20,16},{22,... | collective-permute-start | bytes 5505032 | tf_op jit(solution)/shard_map/ppermute | solution.py:691
  475.1 62.9 %collective-permute-start.2 = (bf16[896,512]{1,0:T(8,128)(2,1)}, bf16[896,512]{1,0:T(8,128)(2,1)}, u32[]{:S(2)}, u32[]{:S(2)}) collective-permute-start(bf16[896,512]{1,0:T(8,128)(2,1)} %get-tuple-element.38), channel_id=1, source_target_pairs={{4,0},{6,2},{8,12},{10,14},{5,1},{7,3},{9,13},{11,15},{20,16},{22,... | collective-permute-start | bytes 2752520 | tf_op jit(solution)/shard_map/ppermute | solution.py:691
  476.4 67.2 %copy-start.1 = (f32[16,1,448]{2,1,0:T(1,128)S(1)}, f32[16,1,448]{2,1,0:T(1,128)}, u32[]{:S(2)}) copy-start(f32[16,1,448]{2,1,0:T(1,128)} %get-tuple-element.48) | copy-start | bytes 86020
  476.4 68.0 %copy-start.2 = (f32[1,3584]{1,0:T(1,128)S(1)}, f32[1,3584]{1,0:T(1,128)}, u32[]{:S(2)}) copy-start(f32[1,3584]{1,0:T(1,128)} %get-tuple-element.45) | copy-start | bytes 43012
  537.9 7.1 %copy-start = (bf16[896,1024]{1,0:T(8,128)(2,1)}, bf16[896,1024]{1,0:T(8,128)(2,1)S(1)}, u32[]{:S(2)}) copy-start(bf16[896,1024]{1,0:T(8,128)(2,1)S(1)} %collective-permute-done.1.got_query) | copy-start | bytes 5505028
  537.9 7.1 %collective-permute-start.3 = (bf16[896,1024]{1,0:T(8,128)(2,1)S(1)}, bf16[896,1024]{1,0:T(8,128)(2,1)}, u32[]{:S(2)}, u32[]{:S(2)}) collective-permute-start(bf16[896,1024]{1,0:T(8,128)(2,1)S(1)} %collective-permute-done.1.got_query), channel_id=1, source_target_pairs={{0,2},{2,0},{12,14},{14,12},{1,3},{3,1},{13,15},{15,13},{16,18},{1... | collective-permute-start | bytes 5505032 | tf_op jit(solution)/shard_map/ppermute | solution.py:694
  539.9 5.2 collective-permute-start.4
  542.3 24.4 %collective-permute-start = (bf16[896,512]{1,0:T(8,128)(2,1)}, bf16[896,512]{1,0:T(8,128)(2,1)S(1)}, u32[]{:S(2)}, u32[]{:S(2)}) collective-permute-start(bf16[896,512]{1,0:T(8,128)(2,1)} %get-tuple-element.32), channel_id=1, source_target_pairs={{4,0},{6,2},{8,12},{10,14},{5,1},{7,3},{9,13},{11,15},{20,16},{22,... | collective-permute-start | bytes 2752520 | tf_op jit(solution)/shard_map/ppermute | solution.py:691
  566.7 4.4 collective-permute-start.5
  571.0 3.7 copy-start.4
  571.0 4.3 copy-start.3
where the time goes:
time: 577 us; the launch traced here: 576 us
  Pallas kernels  527 us (91%)
  waiting for transfers between devices  33.7 us (6%)
  starting transfers between devices  10.1 us (2%)
    pallas_call x1, Pallas kernels, shards(): pl.pallas_call(functools.partial(merge, ranks, widths), out_shape=(shape(...  472 us
    pallas_call x1, Pallas kernels, settled(): pl.pallas_call(settle_kernel, out_shape=(jax.ShapeDtypeStruct(query.shape...  33.8 us
    ppermute x3, waiting for transfers between devices, last_hop(): return lax.ppermute(piece, 'rows', out)  31.3 us
    pallas_call x1, Pallas kernels, blended(): pl.pallas_call(functools.partial(blend_kernel, ranks, wide), out_shape=(j...  18.1 us
  transfers between devices with their start and end apart: 6, of which 3 were waited for; matrix products, arithmetic and copies ran while one was open for 0% of the time, Pallas kernels for 9%

commit v1 on v0

--- a/solution.py
+++ b/solution.py
@@ -13,6 +13,7 @@
 LANES = 128
 LATE = 2
 AHEAD = 3
+PIECES = 4
 
 
 def merge(
@@ -24,7 +25,7 @@
     other_key,
     one_value,
     other_value,
-    mix_row,
+    mix_share,
     norm_train,
     norm_step,
     query,
@@ -36,25 +37,34 @@
     scale_query,
     scale_key,
     scale_value,
-    norms,
+    all_norms,
     one,
     other,
     narrow,
+    mix_row,
     mix,
+    steps,
+    norms,
+    scales,
     peaks,
+    small_sem,
     load_sem,
     out_sem,
+    scale_sem,
     far_sem,
     peak_send,
     peak_recv,
     norm_send,
     norm_recv,
+    wide_send,
+    wide_recv,
     up_send,
     up_recv,
     down_send,
     down_recv,
     side_send,
     side_recv,
+    piece_sems,
 ):
     depth, span = one_key.shape
     parts = one_query.shape[1] // span
@@ -64,7 +74,7 @@
     across = lax.axis_index("width")
     chip, core = me // CORES, me % CORES
     partner = chip * CORES + 1 - core
-    group = ranks * widths
+    last = early - 1
     block = 32 if depth % 32 == 0 else depth
     late_parts = range(early, parts + 2)
 
@@ -86,26 +96,35 @@
         for copy in loads(k):
             copy.start()
 
+    barrier = pltpu.get_barrier_semaphore()
+
+    @pl.loop(1, ranks)
+    def _(step):
+        to = {"rows": lax.rem(me + step, ranks)}
+        pl.semaphore_signal(barrier, inc=1, device_id=to, device_id_type=MESH)
+
+    @pl.loop(1, widths)
+    def _(step):
+        to = {"width": lax.rem(across + step, widths)}
+        pl.semaphore_signal(barrier, inc=1, device_id=to, device_id_type=MESH)
+
+    small = [
+        pltpu.make_async_copy(mix_share, mix_row, small_sem.at[0]),
+        pltpu.make_async_copy(norm_train, steps.at[0], small_sem.at[1]),
+        pltpu.make_async_copy(norm_step, steps.at[1], small_sem.at[2]),
+    ]
+    for copy in small:
+        copy.start()
+
     pl.loop(0, AHEAD)(load)
 
-    barrier = pltpu.get_barrier_semaphore()
-    mine = me * widths + across
-
-    @pl.loop(1, group)
-    def _(step):
-        to = lax.rem(mine + step, group)
-        pl.semaphore_signal(
-            barrier,
-            inc=1,
-            device_id={"rows": to // widths, "width": lax.rem(to, widths)},
-            device_id_type=MESH,
-        )
-
-    norms[mine] = norm_train[...] + norm_step[...]
-
-    for first in range(0, mix.shape[0], LANES):
-        row = mix_row[:, first : first + LANES]
-        mix[first : first + LANES] = jnp.broadcast_to(row, (LANES, LANES)).T
+    for copy in small:
+        copy.wait()
+    norms[across, me] = steps[0] + steps[1]
+
+    for i in range(mix_row.shape[0]):
+        row = jnp.broadcast_to(mix_row[i : i + 1], (LANES, LANES))
+        mix[i * LANES : (i + 1) * LANES] = row.T
 
     def send_peaks(k):
         @pl.loop(1, ranks)
@@ -202,11 +221,18 @@
     def keep(k):
         return pltpu.make_async_copy(narrow.at[k], slot(k, me), out_sem.at[k])
 
-    def scaled(k, scale_ref, cut):
+    def keep_scale(k):
+        if is_tail(k):
+            target = scale_key if k == parts else scale_value
+        else:
+            target = scale_query.at[:, pl.ds(pl.multiple_of(k * span, span), span)]
+        return pltpu.make_async_copy(scales.at[k], target, scale_sem.at[k])
+
+    def scaled(k):
         everyone = peaks.at[k, pl.ds(0, ranks - 1)]
         pltpu.make_async_copy(everyone, everyone, peak_recv.at[k]).wait()
         scale = jnp.max(peaks[k], axis=0)
-        scale_ref[:, cut] = scale
+        scales[k] = scale
 
         @pl.loop(0, depth // block)
         def _(b):
@@ -225,47 +251,53 @@
 
         go_side(k, 0, source).start()
         keep(k).start()
-
-    def part_cut(k):
-        return pl.ds(pl.multiple_of(k * span, span), span)
-
-    mixed(0)
-    pl.semaphore_wait(barrier, group - 1)
-    send_peaks(0)
+        keep_scale(k).start()
+
+    lag = min(3, parts)
+    pl.loop(0, lag)(mixed)
+    pl.semaphore_wait(barrier, ranks + widths - 2)
+    pl.loop(0, lag)(send_peaks)
 
     def advance(k):
         mixed(k)
         send_peaks(k)
 
-    lag = min(2, parts)
-    pl.loop(1, lag)(advance)
-
     @pl.loop(0, parts - lag)
     def _(k):
+        scaled(k)
         advance(k + lag)
-        scaled(k, scale_query, part_cut(k))
 
     advance(parts)
     advance(parts + 1)
 
-    @pl.loop(1, group)
+    @pl.loop(1, ranks)
     def _(step):
-        to = lax.rem(mine + step, group)
         pltpu.make_async_remote_copy(
-            src_ref=norms.at[mine],
-            dst_ref=norms.at[mine],
+            src_ref=norms.at[across, me],
+            dst_ref=norms.at[across, me],
             send_sem=norm_send,
             recv_sem=norm_recv,
-            device_id={"rows": to // widths, "width": lax.rem(to, widths)},
+            device_id={"rows": lax.rem(me + step, ranks)},
             device_id_type=MESH,
         ).start()
 
-    @pl.loop(parts - lag, parts)
-    def _(k):
-        scaled(k, scale_query, part_cut(k))
-
-    scaled(parts, scale_key, slice(None))
-    scaled(parts + 1, scale_value, slice(None))
+    pl.loop(parts - lag, parts)(scaled)
+    scaled(parts)
+    scaled(parts + 1)
+
+    others = norms.at[across, pl.ds(0, ranks - 1)]
+    pltpu.make_async_copy(others, others, norm_recv).wait()
+
+    @pl.loop(1, widths)
+    def _(step):
+        pltpu.make_async_remote_copy(
+            src_ref=norms.at[across],
+            dst_ref=norms.at[across],
+            send_sem=wide_send,
+            recv_sem=wide_recv,
+            device_id={"width": lax.rem(across + step, widths)},
+            device_id_type=MESH,
+        ).start()
 
     def far_copy(k, rank):
         if is_tail(k):
@@ -274,9 +306,41 @@
             target = far_query.at[:, pl.ds((k - early) * span, span)]
         return pltpu.make_async_copy(slot(k, rank), target, far_sem.at[k - early])
 
+    def piece(i, to, rank, kind):
+        rows = pl.ds(i * (depth // PIECES), depth // PIECES)
+        ref = slot(last, rank).at[rows]
+        return pltpu.make_async_remote_copy(
+            src_ref=ref,
+            dst_ref=ref,
+            send_sem=piece_sems.at[2 * kind, i],
+            recv_sem=piece_sems.at[2 * kind + 1, i],
+            device_id={"rows": to},
+            device_id_type=MESH,
+        )
+
+    reach = CORES * (chips - 1)
+
+    def piece_up(i):
+        return piece(i, me + CORES, me + CORES - reach, 0)
+
+    def piece_down(i):
+        return piece(i, me - CORES, me - CORES + reach, 0)
+
+    def each_piece(body):
+        for i in range(PIECES):
+            body(i)
+
+    def last_hop(rank):
+        def body(i):
+            piece(i, partner, rank, 0).wait_recv()
+            piece(i, partner, rank, 1).start()
+
+        each_piece(body)
+
     def relay(k, hop):
-        onward = hop < hops(k)
         is_far = is_static(k) and k >= early
+        is_last = is_static(k) and k == last
+        onward = hop < (chips - 2 if is_last else hops(k))
 
         @pl.when(chip >= hop)
         def _():
@@ -288,6 +352,12 @@
 
             go_side(k, -hop).start()
 
+            if is_last:
+
+                @pl.when((hop == chips - 2) & has_above)
+                def _():
+                    each_piece(lambda i: piece_up(i).start())
+
             if is_far:
 
                 @pl.when((hop == chips - 2) & (chip == chips - 2))
@@ -304,6 +374,12 @@
 
             go_side(k, hop).start()
 
+            if is_last:
+
+                @pl.when((hop == chips - 2) & has_below)
+                def _():
+                    each_piece(lambda i: piece_down(i).start())
+
             if is_far:
 
                 @pl.when((hop == chips - 2) & (chip == 1))
@@ -312,16 +388,17 @@
 
     @pl.loop(1, chips - 1)
     def _(hop):
-        pl.loop(0, early)(lambda k: relay(k, hop))
+        pl.loop(0, last)(lambda k: relay(k, hop))
+        relay(last, hop)
         for k in late_parts:
             relay(k, hop)
 
-    pl.loop(0, early)(lambda k: relay(k, chips - 1))
-
     def finish(k):
         keep(k).wait()
-
-        @pl.loop(0, hops(k))
+        keep_scale(k).wait()
+        most = chips - 2 if is_static(k) else chips - 1
+
+        @pl.loop(0, most)
         def _(hop):
             @pl.when((chip >= hop) & has_above)
             def _():
@@ -333,29 +410,62 @@
 
         @pl.loop(0, chips)
         def _(origin):
-            @pl.when((origin - chip <= hops(k)) & (chip - origin <= hops(k)))
+            @pl.when((origin - chip <= most) & (chip - origin <= most))
             def _():
                 go_side(k, origin - chip).wait_send()
                 from_side(k, origin - chip).wait_recv()
 
-        if is_static(k):
-
-            @pl.when((chip == 1) | (chip == chips - 2))
-            def _():
-                far_copy(k, me).wait()
-
-    for k in late_parts:
-        finish(k)
-
     def settle(k):
         everyone = peaks.at[k, pl.ds(0, ranks - 1)]
         pltpu.make_async_copy(everyone, everyone, peak_send.at[k]).wait()
 
+    for k in late_parts:
+        finish(k)
+
+        @pl.when((chip == 1) | (chip == chips - 2))
+        def _():
+            far_copy(k, me).wait()
+
+    finish(last)
     pl.loop(0, parts + 2)(settle)
-    others = norms.at[pl.ds(0, group - 1)]
-    pltpu.make_async_copy(others, others, norm_recv).wait()
     pltpu.make_async_copy(others, others, norm_send).wait()
-    pl.loop(0, early)(finish)
+    around = norms.at[pl.ds(0, widths - 1)]
+    pltpu.make_async_copy(around, around, wide_recv).wait()
+    pltpu.make_async_copy(around, around, wide_send).wait()
+    keep_norms = pltpu.make_async_copy(norms, all_norms, small_sem.at[3])
+    keep_norms.start()
+    keep_norms.wait()
+
+    @pl.loop(0, last)
+    def _(k):
+        relay(k, chips - 1)
+
+        @pl.when(k > 0)
+        def _():
+            finish(k - 1)
+
+    if last > 0:
+        finish(jnp.int32(last - 1))
+
+    @pl.when(chip == chips - 1)
+    def _():
+        last_hop(me - reach)
+
+    @pl.when(chip == 0)
+    def _():
+        last_hop(me + reach)
+
+    @pl.when((chip == 0) | (chip == chips - 1))
+    def _():
+        def body(i):
+            piece(i, partner, me, 1).wait_send()
+            piece(i, partner, me, 1).wait_recv()
+
+        each_piece(body)
+
+    @pl.when((chip == 1) | (chip == chips - 2))
+    def _():
+        each_piece(lambda i: piece(i, partner, me, 0).wait_send())
 
 
 def stream(total, incoming, outgoing, ring):
@@ -394,7 +504,20 @@
         copy.wait()
 
 
-def settle_kernel(query, value, new_query, new_value, done, wide_buf, slim_buf, sems):
+def settle_kernel(
+    query,
+    value,
+    scale_key,
+    scale_value,
+    new_query,
+    new_value,
+    new_scale_key,
+    new_scale_value,
+    done,
+    wide_buf,
+    slim_buf,
+    sems,
+):
     ring = wide_buf.shape[0]
 
     def plan(source, target, buf, at):
@@ -429,6 +552,8 @@
     second[1]()
     first[2]()
     second[2]()
+    new_scale_key[...] = scale_key[...]
+    new_scale_value[...] = scale_value[...]
     done[...] = jnp.zeros_like(done)
 
 
@@ -439,21 +564,24 @@
     return step
 
 
-def settled(query, value, wide, ring=8):
+def settled(query, value, scale_key, scale_value, wide, ring=8):
     rows, span = value.shape
     step = chunk_of(rows, 128)
     slim = chunk_of(rows, 512)
     anywhere = pl.BlockSpec(memory_space=pl.ANY)
+    near = pl.BlockSpec(memory_space=pltpu.VMEM)
     moved = 4 * rows * (wide + span)
     return pl.pallas_call(
         settle_kernel,
         out_shape=(
             jax.ShapeDtypeStruct(query.shape, query.dtype),
             jax.ShapeDtypeStruct(value.shape, value.dtype),
+            jax.ShapeDtypeStruct(scale_key.shape, scale_key.dtype),
+            jax.ShapeDtypeStruct(scale_value.shape, scale_value.dtype),
             jax.ShapeDtypeStruct((8, LANES), jnp.float32),
         ),
-        in_specs=[anywhere] * 2,
-        out_specs=(anywhere, anywhere, pl.BlockSpec(memory_space=pltpu.VMEM)),
+        in_specs=[anywhere, anywhere, near, near],
+        out_specs=(anywhere, anywhere, near, near, near),
         scratch_shapes=[
             pltpu.VMEM((ring, step, wide), query.dtype),
             pltpu.VMEM((ring, slim, span), value.dtype),
@@ -463,7 +591,7 @@
         cost_estimate=pl.CostEstimate(
             flops=0, bytes_accessed=moved, transcendentals=0
         ),
-    )(query, value)
+    )(query, value, scale_key, scale_value)
 
 
 def far_ranks(ranks):
@@ -475,125 +603,87 @@
     return at_end, away + core, away + 1 - core
 
 
-def blend_kernel(
-    ranks, wide, _, query, key, got_query, side_query, got_key, side_key, done,
-    new_query, new_key, query_buf, key_buf, sems,
-):
-    depth = got_key.shape[0]
+def blend_kernel(ranks, first, fresh, whole, got, side, done, target, buf, sems):
     at_end, straight, crossed = far_ranks(ranks)
-    ring = query_buf.shape[0]
-    late = query_buf.shape[2]
-
-    def plan(source, got, side, target, buf, cols, at):
-        def rows(i):
-            return pl.ds(pl.multiple_of(i * depth, depth), depth)
-
-        def incoming(i, begin):
-            place = lax.rem(i, ring)
-
-            def copy(origin):
-                act(pltpu.make_async_copy(origin, buf.at[place], sems.at[at, place]), begin)
-
-            if not begin:
-                copy(source.at[rows(i), cols])
-                return
-            is_got = at_end & (i == straight)
-            is_side = at_end & (i == crossed)
-            pl.when(is_got)(lambda: copy(got))
-            pl.when(is_side)(lambda: copy(side))
-            pl.when(jnp.logical_not(is_got | is_side))(lambda: copy(source.at[rows(i), cols]))
-
-        def outgoing(i):
-            place = lax.rem(i, ring)
-            return pltpu.make_async_copy(
-                buf.at[place], target.at[rows(i), cols], sems.at[at + 1, place]
-            )
-
-        return stream(ranks, incoming, outgoing, ring)
-
-    first = plan(
-        query, got_query, side_query, new_query, query_buf, pl.ds(wide, late), 0
-    )
-    second = plan(key, got_key, side_key, new_key, key_buf, pl.ds(0, key_buf.shape[2]), 2)
-    first[0]()
-    second[0]()
-    first[1]()
-    second[1]()
-    first[2]()
-    second[2]()
-
-
-def blended(
-    ranks, wide, new_query, query, key, got_query, side_query, got_key, side_key, done, ring=4
-):
-    depth, span = got_key.shape
-    late = got_query.shape[1]
+    ring, depth, span = buf.shape
+    cols = pl.ds(first, span)
+
+    def rows(i):
+        return pl.ds(pl.multiple_of(i * depth, depth), depth)
+
+    def incoming(i, begin):
+        place = lax.rem(i, ring)
+
+        def copy(origin):
+            act(pltpu.make_async_copy(origin, buf.at[place], sems.at[0, place]), begin)
+
+        if not begin:
+            copy(whole.at[rows(i), cols])
+            return
+        is_got = at_end & (i == straight)
+        is_side = at_end & (i == crossed)
+        pl.when(is_got)(lambda: copy(got))
+        pl.when(is_side)(lambda: copy(side))
+        pl.when(jnp.logical_not(is_got | is_side))(lambda: copy(whole.at[rows(i), cols]))
+
+    def outgoing(i):
+        place = lax.rem(i, ring)
+        return pltpu.make_async_copy(buf.at[place], target.at[rows(i), cols], sems.at[1, place])
+
+    for phase in stream(ranks, incoming, outgoing, ring):
+        phase()
+
+
+def blended(ranks, first, fresh, whole, got, side, done, ring=6):
     anywhere = pl.BlockSpec(memory_space=pl.ANY)
-    moved = 4 * ranks * depth * (late + span)
     return pl.pallas_call(
-        functools.partial(blend_kernel, ranks, wide),
-        out_shape=(
-            jax.ShapeDtypeStruct(query.shape, query.dtype),
-            jax.ShapeDtypeStruct(key.shape, key.dtype),
-        ),
-        in_specs=[anywhere] * 8,
-        out_specs=(anywhere, anywhere),
+        functools.partial(blend_kernel, ranks, first),
+        out_shape=jax.ShapeDtypeStruct(whole.shape, whole.dtype),
+        in_specs=[anywhere] * 5,
+        out_specs=anywhere,
         scratch_shapes=[
-            pltpu.VMEM((ring, depth, late), query.dtype),
-            pltpu.VMEM((ring, depth, span), key.dtype),
-            pltpu.SemaphoreType.DMA((4, ring)),
+            pltpu.VMEM((ring, *got.shape), whole.dtype),
+            pltpu.SemaphoreType.DMA((2, ring)),
         ],
-        input_output_aliases={0: 0},
+        input_output_aliases={} if fresh is done else {0: 0},
         compiler_params=pltpu.CompilerParams(vmem_limit_bytes=60 * 2**20),
         cost_estimate=pl.CostEstimate(
-            flops=0, bytes_accessed=moved, transcendentals=0
+            flops=0, bytes_accessed=4 * ranks * got.size, transcendentals=0
         ),
-    )(new_query, query, key, got_query, side_query, got_key, side_key, done)
-
-
-def place_kernel(ranks, _, got, side, target, buf, sems):
+    )(fresh, whole, got, side, done)
+
+
+def place_kernel(ranks, _, got, side, target, sems):
     at_end, straight, crossed = far_ranks(ranks)
     depth = got.shape[0]
-    step = buf.shape[1]
-    cuts = depth // step
 
     @pl.when(at_end)
     def _():
-        def incoming(i):
-            source = (got, side)[i // cuts]
-            rows = pl.ds(i % cuts * step, step)
-            return pltpu.make_async_copy(source.at[rows], buf.at[i], sems.at[0, i])
-
-        def outgoing(i):
-            rank = (straight, crossed)[i // cuts]
-            rows = pl.ds(pl.multiple_of(rank * depth + i % cuts * step, step), step)
-            return pltpu.make_async_copy(buf.at[i], target.at[rows], sems.at[1, i])
-
-        for i in range(2 * cuts):
-            incoming(i).start()
-        for i in range(2 * cuts):
-            incoming(i).wait()
-            outgoing(i).start()
-        for i in range(2 * cuts):
-            outgoing(i).wait()
-
-
-def placed(ranks, whole, got, side, cuts=4):
-    depth, span = got.shape
+        copies = [
+            pltpu.make_async_copy(
+                source, target.at[pl.ds(pl.multiple_of(rank * depth, depth), depth)], sems.at[i]
+            )
+            for i, (source, rank) in enumerate(((got, straight), (side, crossed)))
+        ]
+        for copy in copies:
+            copy.start()
+        for copy in copies:
+            copy.wait()
+
+
+def placed(ranks, whole, got, side):
     anywhere = pl.BlockSpec(memory_space=pl.ANY)
+    near = pl.BlockSpec(memory_space=pltpu.VMEM)
     return pl.pallas_call(
         functools.partial(place_kernel, ranks),
         out_shape=jax.ShapeDtypeStruct(whole.shape, whole.dtype),
-        in_specs=[anywhere] * 3,
+        in_specs=[anywhere, near, near],
         out_specs=anywhere,
-        scratch_shapes=[
-            pltpu.VMEM((2 * cuts, depth // cuts, span), whole.dtype),
-            pltpu.SemaphoreType.DMA((2, 2 * cuts)),
-        ],
+        scratch_shapes=[pltpu.SemaphoreType.DMA((2,))],
         input_output_aliases={0: 0},
         compiler_params=pltpu.CompilerParams(vmem_limit_bytes=8 * 2**20),
         cost_estimate=pl.CostEstimate(
-            flops=0, bytes_accessed=8 * depth * span, transcendentals=0
+            flops=0, bytes_accessed=4 * got.size, transcendentals=0
         ),
     )(whole, got, side)
 
@@ -615,16 +705,14 @@
     wide = one_query.shape[1]
     parts = wide // span
     chips = ranks // CORES
-    group = ranks * widths
     bit = norm_train.shape[0]
     late = LATE * span
     tall = -(-depth // LANES) * LANES
-    mix_row = mix_share[None]
     if tall != depth:
-        mix_row = jnp.pad(mix_row, ((0, 0), (0, tall - depth)))
+        mix_share = jnp.pad(mix_share, (0, tall - depth))
+    mix_rows = mix_share.reshape(tall // LANES, LANES)
     shape = jax.ShapeDtypeStruct
     anywhere = pl.BlockSpec(memory_space=pl.ANY)
-    near = pl.BlockSpec(memory_space=pltpu.VMEM)
     dma = pltpu.SemaphoreType.DMA
     (
         query, key, value, far_query, far_key, far_value,
@@ -641,21 +729,29 @@
             shape((1, wide), jnp.float32),
             shape((1, span), jnp.float32),
             shape((1, span), jnp.float32),
-            shape((group, 1, bit), jnp.float32),
+            shape((widths, ranks, 1, bit), jnp.float32),
         ),
-        in_specs=[anywhere] * 6 + [near] * 3,
-        out_specs=[anywhere] * 6 + [near] * 4,
+        in_specs=[anywhere] * 9,
+        out_specs=[anywhere] * 10,
         scratch_shapes=[
             pltpu.VMEM((parts + 2, depth, span), jnp.float32),
             pltpu.VMEM((parts + 2, depth, span), jnp.float32),
             pltpu.VMEM((parts + 2, depth, span), jnp.bfloat16),
+            pltpu.VMEM(mix_rows.shape, jnp.float32),
             pltpu.VMEM((tall, LANES), jnp.float32),
+            pltpu.VMEM((2, 1, bit), jnp.float32),
+            pltpu.VMEM((widths, ranks, 1, bit), jnp.float32),
+            pltpu.VMEM((parts + 2, 1, span), jnp.float32),
             pltpu.VMEM((parts + 2, ranks, 1, span), jnp.float32),
+            dma((4,)),
             dma((2, parts + 2)),
+            dma((parts + 2,)),
             dma((parts + 2,)),
             dma((LATE + 2,)),
             dma((parts + 2,)),
             dma((parts + 2,)),
+            dma,
+            dma,
             dma,
             dma,
             dma((chips - 1, parts + 2)),
@@ -664,6 +760,7 @@
             dma((chips - 1, parts + 2)),
             dma((2 * chips - 1, parts + 2)),
             dma((2 * chips - 1, parts + 2)),
+            dma((4, PIECES)),
         ],
         compiler_params=pltpu.CompilerParams(
             collective_id=0, has_side_effects=True, vmem_limit_bytes=56 * 2**20
@@ -675,7 +772,7 @@
         other_key,
         one_value,
         other_value,
-        mix_row,
+        mix_rows,
         norm_train[None],
         norm_step[None],
     )
@@ -696,21 +793,22 @@
     got_query = last_hop(far_query)
     got_key = last_hop(far_key)
     got_value = last_hop(far_value)
-    new_query, new_value, done = settled(query, value, wide - late)
+    new_query, new_value, scale_key, scale_value, done = settled(
+        query, value, scale_key, scale_value, wide - late
+    )
     small = (
         scale_query[0],
         scale_key[0],
         scale_value[0],
-        norms.reshape(-1).astype(jnp.bfloat16),
+        norms.transpose(1, 0, 2, 3).reshape(-1).astype(jnp.bfloat16),
     )
-    got_query, got_key, done = lax.optimization_barrier((got_query, got_key, done))
-    side_query, side_key = to_side(got_query), to_side(got_key)
-    new_query, new_key = blended(
-        ranks, wide - late, new_query, query, key, got_query, side_query, got_key, side_key, done
+    got_query, done = lax.optimization_barrier((got_query, done))
+    new_query = blended(
+        ranks, wide - late, new_query, query, got_query, to_side(got_query), done
     )
-    got_value, new_query, new_key, small = lax.optimization_barrier(
-        (got_value, new_query, new_key, small)
-    )
+    got_key, new_query = lax.optimization_barrier((got_key, new_query))
+    new_key = blended(ranks, 0, done, key, got_key, to_side(got_key), done)
+    got_value, new_key, small = lax.optimization_barrier((got_value, new_key, small))
     new_value = placed(ranks, new_value, got_value, to_side(got_value))
     return (new_query, new_key, new_value, *small)
 
@@ -738,4 +836,6 @@
     )
     body = functools.partial(shards, mesh.shape["rows"], mesh.shape["width"])
 
-    return jax.shard_map(body, mesh=mesh, in_specs=in_specs, out_specs=out_specs, check_vma=False)
+    return jax.shard_map(
+        body, mesh=mesh, in_specs=in_specs, out_specs=out_specs, check_vma=False
+    )

time: 577 us -> 578 us (level)
    pallas_call x1 -> x2, Pallas kernels: 18.1 us -> 17.5 us  [blended(): pl.pallas_call(functools.partial(blend_kernel, ranks, first), out_shape=j...]
  transfers between devices with their start and end apart: 6 -> 6, of which waited for: 3 -> 5; matrix products, arithmetic and copies ran while one was open for 0% -> 0% of each run, Pallas kernels for 9% -> 9%
where the time goes in v1:
time: 578 us; the launch traced here: 576 us
  Pallas kernels  525 us (91%)
  waiting for transfers between devices  37.2 us (6%)
  starting transfers between devices  9.6 us (2%)
    pallas_call x1, Pallas kernels, shards(): pl.pallas_call(functools.partial(merge, ranks, widths), out_shape=(shape(...  472 us
    pallas_call x1, Pallas kernels, settled(): pl.pallas_call(settle_kernel, out_shape=(jax.ShapeDtypeStruct(query.shape...  34.5 us
    ppermute x3, waiting for transfers between devices, last_hop(): return lax.ppermute(piece, 'rows', out)  32.3 us
    pallas_call x2, Pallas kernels, blended(): pl.pallas_call(functools.partial(blend_kernel, ranks, first), out_shape=j...  17.5 us
  transfers between devices with their start and end apart: 6, of which 5 were waited for; matrix products, arithmetic and copies ran while one was open for 0% of the time, Pallas kernels for 9%

profile of v1, /device:TPU:0, one launch (start us, length us, event | category | flops | bytes accessed | tf_op | source)
XLA Modules:
  0.0 576.3 jit_solution(16088737618603692918)
XLA Ops:
  0.6 472.0 %shard_map.144 = (bf16[7168,3584]{1,0:T(8,128)(2,1)}, bf16[7168,512]{1,0:T(8,128)(2,1)}, bf16[7168,512]{1,0:T(8,128)(2,1)}, bf16[896,1024]{1,0:T(8,128)(2,1)}, b...) custom-call(f32[896,3584]{1,0:T(8,128)} %one_query.1, ...), custom_call_target="tpu_custom_call" | custom-call | tf_op jit(solution)/shard_map/pallas_call | solution.py:720
  472.6 1.3 collective-permute-start.1
  473.9 34.5 %shard_map.145 = (bf16[7168,3584]{1,0:T(8,128)(2,1)}, bf16[7168,512]{1,0:T(8,128)(2,1)}, f32[1,512]{1,0:T(1,128)}, f32[1,512]{1,0:T(1,128)}, f32[8,128]{1,0:T(8,128)}) custom-call(bf16[7168,3584]{1,0:T(8,128)(2,1)} %get-tuple-element.33.query.whole, bf16[7168,512]{1,0:T(8,128)(2,1)} %get-tuple-element.34.value, f32[1,512]{1,0:T(1,128)} %get-tuple-element.35.scale_key, ...), custom_call_target="tpu_custom_call" | custom-call | bytes 88080384 | tf_op jit(solution)/shard_map/pallas_call | solution.py:574
  508.4 8.6 %collective-permute-done.1.got = bf16[896,1024]{1,0:T(8,128)(2,1)S(1)} collective-permute-done((bf16[896,1024]{1,0:T(8,128)(2,1)}, bf16[896,1024]{1,0:T(8,128)(2,1)S(1)}, u32[]{:S(2)}, u32[]{:S(2)}) %collective-permute-start.1) | collective-permute-done | bytes 1835040 | tf_op jit(solution)/shard_map/ppermute | solution.py:788
  517.0 0.0 copy-start
  517.0 1.9 collective-permute-start.2
  518.9 1.3 collective-permute-start
  520.2 2.5 collective-permute-done.2.side
  522.7 0.0 copy-start.1
  522.7 0.0 copy-done
  522.7 1.3 copy-done.1
  523.9 0.0 copy-start.3
  523.9 0.0 copy-start.4
  523.9 10.8 %shard_map.146 = bf16[7168,3584]{1,0:T(8,128)(2,1)} custom-call(bf16[7168,3584]{1,0:T(8,128)(2,1)} %get-tuple-element.37.fresh, bf16[7168,3584]{1,0:T(8,128)(2,1)} %get-tuple-element.33.query.whole, bf16[896,1024]{1,0:T(8,128)(2,1)} %copy-done, bf16[896,1024]{1,0:T(8,128)(2,1)} %copy-done.1, ...), custom_call_target="tpu_custom_call", output_to_operand_aliasing={{}: (0, {})} | custom-call | bytes 29360128 | tf_op jit(solution)/shard_map/pallas_call | solution.py:639
  534.8 9.1 %collective-permute-done.got = bf16[896,512]{1,0:T(8,128)(2,1)} collective-permute-done((bf16[896,512]{1,0:T(8,128)(2,1)}, bf16[896,512]{1,0:T(8,128)(2,1)}, u32[]{:S(2)}, u32[]{:S(2)}) %collective-permute-start) | collective-permute-done | bytes 917536 | tf_op jit(solution)/shard_map/ppermute | solution.py:788
  543.9 1.9 collective-permute-start.4
  545.8 1.3 collective-permute-start.3
  547.1 0.0 copy-done.3
  547.2 0.7 convert_element_type.11
  547.9 0.0 copy-done.4
  547.9 0.6 reduce
  548.5 0.0 collective-permute-done.4.side
  548.5 0.0 copy-start.2
  548.5 0.9 copy-done.2
  549.5 6.7 %shard_map.147 = bf16[7168,512]{1,0:T(8,128)(2,1)} custom-call(f32[8,128]{1,0:T(8,128)} %get-tuple-element.41.done.fresh, bf16[7168,512]{1,0:T(8,128)(2,1)} %get-tuple-element.44.whole, bf16[896,512]{1,0:T(8,128)(2,1)} %collective-permute-done.got, bf16[896,512]{1,0:T(8,128)(2,1)} %copy-done.2, f32[8,128]{1,0:T(8,128)} %get-tuple-element.41.done.fresh), custom_call_target="tpu_custom_call" | custom-call | bytes 14680064 | tf_op jit(solution)/shard_map/pallas_call | solution.py:639
  556.1 14.5 %collective-permute-done.3.got = bf16[896,512]{1,0:T(8,128)(2,1)S(1)} collective-permute-done((bf16[896,512]{1,0:T(8,128)(2,1)}, bf16[896,512]{1,0:T(8,128)(2,1)S(1)}, u32[]{:S(2)}, u32[]{:S(2)}) %collective-permute-start.3) | collective-permute-done | bytes 917536 | tf_op jit(solution)/shard_map/ppermute | solution.py:788
  570.7 1.9 collective-permute-start.5
  572.6 2.4 collective-permute-done.5.side
  575.0 1.2 shard_map.148
  (2 shorter events, 0.1 us)
Async XLA Ops:
  472.6 44.4 %collective-permute-start.1 = (bf16[896,1024]{1,0:T(8,128)(2,1)}, bf16[896,1024]{1,0:T(8,128)(2,1)S(1)}, u32[]{:S(2)}, u32[]{:S(2)}) collective-permute-start(bf16[896,1024]{1,0:T(8,128)(2,1)} %get-tuple-element.38), channel_id=1, source_target_pairs={{4,0},{6,2},{8,12},{10,14},{5,1},{7,3},{9,13},{11,15},{20,16},{22,... | collective-permute-start | bytes 5505032 | tf_op jit(solution)/shard_map/ppermute | solution.py:788
  517.0 5.7 copy-start
  517.0 5.7 collective-permute-start.2
  518.9 25.0 %collective-permute-start = (bf16[896,512]{1,0:T(8,128)(2,1)}, bf16[896,512]{1,0:T(8,128)(2,1)}, u32[]{:S(2)}, u32[]{:S(2)}) collective-permute-start(bf16[896,512]{1,0:T(8,128)(2,1)} %get-tuple-element.32), channel_id=1, source_target_pairs={{4,0},{6,2},{8,12},{10,14},{5,1},{7,3},{9,13},{11,15},{20,16},{22,... | collective-permute-start | bytes 2752520 | tf_op jit(solution)/shard_map/ppermute | solution.py:788
  522.7 1.3 copy-start.1
  523.9 23.2 %copy-start.3 = (f32[2,8,1,448]{3,2,1,0:T(1,128)S(1)}, f32[2,8,1,448]{3,2,1,0:T(1,128)}, u32[]{:S(2)}) copy-start(f32[2,8,1,448]{3,2,1,0:T(1,128)} %get-tuple-element.49) | copy-start | bytes 86020
  523.9 23.9 %copy-start.4 = (f32[1,3584]{1,0:T(1,128)S(1)}, f32[1,3584]{1,0:T(1,128)}, u32[]{:S(2)}) copy-start(f32[1,3584]{1,0:T(1,128)} %get-tuple-element.46) | copy-start | bytes 43012
  543.9 4.6 collective-permute-start.4
  545.8 24.9 %collective-permute-start.3 = (bf16[896,512]{1,0:T(8,128)(2,1)}, bf16[896,512]{1,0:T(8,128)(2,1)S(1)}, u32[]{:S(2)}, u32[]{:S(2)}) collective-permute-start(bf16[896,512]{1,0:T(8,128)(2,1)} %get-tuple-element.43), channel_id=1, source_target_pairs={{4,0},{6,2},{8,12},{10,14},{5,1},{7,3},{9,13},{11,15},{20,16},{22,... | collective-permute-start | bytes 2752520 | tf_op jit(solution)/shard_map/ppermute | solution.py:788
  548.5 0.9 copy-start.2
  570.7 4.4 collective-permute-start.5

commit v2 on v1

--- a/solution.py
+++ b/solution.py
@@ -13,7 +13,6 @@
 LANES = 128
 LATE = 2
 AHEAD = 3
-PIECES = 4
 
 
 def merge(
@@ -31,6 +30,7 @@
     query,
     key,
     value,
+    far_early,
     far_query,
     far_key,
     far_value,
@@ -64,7 +64,8 @@
     down_recv,
     side_send,
     side_recv,
-    piece_sems,
+    early_send,
+    early_recv,
 ):
     depth, span = one_key.shape
     parts = one_query.shape[1] // span
@@ -302,43 +303,24 @@
     def far_copy(k, rank):
         if is_tail(k):
             target = far_key if k == parts else far_value
+        elif k == last:
+            target = far_early
         else:
             target = far_query.at[:, pl.ds((k - early) * span, span)]
-        return pltpu.make_async_copy(slot(k, rank), target, far_sem.at[k - early])
-
-    def piece(i, to, rank, kind):
-        rows = pl.ds(i * (depth // PIECES), depth // PIECES)
-        ref = slot(last, rank).at[rows]
+        return pltpu.make_async_copy(slot(k, rank), target, far_sem.at[k - last])
+
+    def last_early(rank, to):
         return pltpu.make_async_remote_copy(
-            src_ref=ref,
-            dst_ref=ref,
-            send_sem=piece_sems.at[2 * kind, i],
-            recv_sem=piece_sems.at[2 * kind + 1, i],
+            src_ref=slot(last, rank),
+            dst_ref=far_early,
+            send_sem=early_send,
+            recv_sem=early_recv,
             device_id={"rows": to},
             device_id_type=MESH,
         )
 
-    reach = CORES * (chips - 1)
-
-    def piece_up(i):
-        return piece(i, me + CORES, me + CORES - reach, 0)
-
-    def piece_down(i):
-        return piece(i, me - CORES, me - CORES + reach, 0)
-
-    def each_piece(body):
-        for i in range(PIECES):
-            body(i)
-
-    def last_hop(rank):
-        def body(i):
-            piece(i, partner, rank, 0).wait_recv()
-            piece(i, partner, rank, 1).start()
-
-        each_piece(body)
-
     def relay(k, hop):
-        is_far = is_static(k) and k >= early
+        is_far = is_static(k)
         is_last = is_static(k) and k == last
         onward = hop < (chips - 2 if is_last else hops(k))
 
@@ -354,9 +336,9 @@
 
             if is_last:
 
-                @pl.when((hop == chips - 2) & has_above)
+                @pl.when((hop == chips - 2) & has_above & (core == 1))
                 def _():
-                    each_piece(lambda i: piece_up(i).start())
+                    last_early(me - CORES * hop, me + CORES).start()
 
             if is_far:
 
@@ -376,9 +358,9 @@
 
             if is_last:
 
-                @pl.when((hop == chips - 2) & has_below)
+                @pl.when((hop == chips - 2) & has_below & (core == 1))
                 def _():
-                    each_piece(lambda i: piece_down(i).start())
+                    last_early(me + CORES * hop, me - CORES).start()
 
             if is_far:
 
@@ -419,14 +401,16 @@
         everyone = peaks.at[k, pl.ds(0, ranks - 1)]
         pltpu.make_async_copy(everyone, everyone, peak_send.at[k]).wait()
 
-    for k in late_parts:
+    near_end = (chip == 1) | (chip == chips - 2)
+    at_end = (chip == 0) | (chip == chips - 1)
+
+    for k in (last, *late_parts):
         finish(k)
 
-        @pl.when((chip == 1) | (chip == chips - 2))
+        @pl.when(near_end)
         def _():
             far_copy(k, me).wait()
 
-    finish(last)
     pl.loop(0, parts + 2)(settle)
     pltpu.make_async_copy(others, others, norm_send).wait()
     around = norms.at[pl.ds(0, widths - 1)]
@@ -447,25 +431,13 @@
     if last > 0:
         finish(jnp.int32(last - 1))
 
-    @pl.when(chip == chips - 1)
+    @pl.when(at_end & (core == 1))
     def _():
-        last_hop(me - reach)
-
-    @pl.when(chip == 0)
+        last_early(me, partner).wait_recv()
+
+    @pl.when(near_end & (core == 1))
     def _():
-        last_hop(me + reach)
-
-    @pl.when((chip == 0) | (chip == chips - 1))
-    def _():
-        def body(i):
-            piece(i, partner, me, 1).wait_send()
-            piece(i, partner, me, 1).wait_recv()
-
-        each_piece(body)
-
-    @pl.when((chip == 1) | (chip == chips - 2))
-    def _():
-        each_piece(lambda i: piece(i, partner, me, 0).wait_send())
+        last_early(me, partner).wait_send()
 
 
 def stream(total, incoming, outgoing, ring):
@@ -566,7 +538,7 @@
 
 def settled(query, value, scale_key, scale_value, wide, ring=8):
     rows, span = value.shape
-    step = chunk_of(rows, 128)
+    step = chunk_of(rows, 256)
     slim = chunk_of(rows, 512)
     anywhere = pl.BlockSpec(memory_space=pl.ANY)
     near = pl.BlockSpec(memory_space=pltpu.VMEM)
@@ -603,8 +575,9 @@
     return at_end, away + core, away + 1 - core
 
 
-def blend_kernel(ranks, first, fresh, whole, got, side, done, target, buf, sems):
+def blend_kernel(ranks, first, fresh, whole, got0, got1, side0, side1, done, target, buf, sems):
     at_end, straight, crossed = far_ranks(ranks)
+    core = lax.axis_index("rows") % CORES
     ring, depth, span = buf.shape
     cols = pl.ds(first, span)
 
@@ -622,35 +595,39 @@
             return
         is_got = at_end & (i == straight)
         is_side = at_end & (i == crossed)
-        pl.when(is_got)(lambda: copy(got))
-        pl.when(is_side)(lambda: copy(side))
+        pl.when(is_got & (core == 0))(lambda: copy(got0))
+        pl.when(is_got & (core == 1))(lambda: copy(got1))
+        pl.when(is_side & (core == 0))(lambda: copy(side0))
+        pl.when(is_side & (core == 1))(lambda: copy(side1))
         pl.when(jnp.logical_not(is_got | is_side))(lambda: copy(whole.at[rows(i), cols]))
 
     def outgoing(i):
         place = lax.rem(i, ring)
-        return pltpu.make_async_copy(buf.at[place], target.at[rows(i), cols], sems.at[1, place])
+        return pltpu.make_async_copy(
+            buf.at[place], target.at[rows(i), cols], sems.at[1, place]
+        )
 
     for phase in stream(ranks, incoming, outgoing, ring):
         phase()
 
 
-def blended(ranks, first, fresh, whole, got, side, done, ring=6):
+def blended(ranks, first, fresh, whole, gots, sides, done, ring=6):
     anywhere = pl.BlockSpec(memory_space=pl.ANY)
     return pl.pallas_call(
         functools.partial(blend_kernel, ranks, first),
         out_shape=jax.ShapeDtypeStruct(whole.shape, whole.dtype),
-        in_specs=[anywhere] * 5,
+        in_specs=[anywhere] * 7,
         out_specs=anywhere,
         scratch_shapes=[
-            pltpu.VMEM((ring, *got.shape), whole.dtype),
+            pltpu.VMEM((ring, *gots[0].shape), whole.dtype),
             pltpu.SemaphoreType.DMA((2, ring)),
         ],
         input_output_aliases={} if fresh is done else {0: 0},
         compiler_params=pltpu.CompilerParams(vmem_limit_bytes=60 * 2**20),
         cost_estimate=pl.CostEstimate(
-            flops=0, bytes_accessed=4 * ranks * got.size, transcendentals=0
+            flops=0, bytes_accessed=4 * ranks * gots[0].size, transcendentals=0
         ),
-    )(fresh, whole, got, side, done)
+    )(fresh, whole, *gots, *sides, done)
 
 
 def place_kernel(ranks, _, got, side, target, sems):
@@ -715,7 +692,7 @@
     anywhere = pl.BlockSpec(memory_space=pl.ANY)
     dma = pltpu.SemaphoreType.DMA
     (
-        query, key, value, far_query, far_key, far_value,
+        query, key, value, far_early, far_query, far_key, far_value,
         scale_query, scale_key, scale_value, norms,
     ) = pl.pallas_call(
         functools.partial(merge, ranks, widths),
@@ -723,6 +700,7 @@
             shape((ranks * depth, wide), jnp.bfloat16),
             shape((ranks * depth, span), jnp.bfloat16),
             shape((ranks * depth, span), jnp.bfloat16),
+            shape((depth, span), jnp.bfloat16),
             shape((depth, late), jnp.bfloat16),
             shape((depth, span), jnp.bfloat16),
             shape((depth, span), jnp.bfloat16),
@@ -732,7 +710,7 @@
             shape((widths, ranks, 1, bit), jnp.float32),
         ),
         in_specs=[anywhere] * 9,
-        out_specs=[anywhere] * 10,
+        out_specs=[anywhere] * 11,
         scratch_shapes=[
             pltpu.VMEM((parts + 2, depth, span), jnp.float32),
             pltpu.VMEM((parts + 2, depth, span), jnp.float32),
@@ -747,7 +725,7 @@
             dma((2, parts + 2)),
             dma((parts + 2,)),
             dma((parts + 2,)),
-            dma((LATE + 2,)),
+            dma((LATE + 3,)),
             dma((parts + 2,)),
             dma((parts + 2,)),
             dma,
@@ -760,7 +738,8 @@
             dma((chips - 1, parts + 2)),
             dma((2 * chips - 1, parts + 2)),
             dma((2 * chips - 1, parts + 2)),
-            dma((4, PIECES)),
+            dma,
+            dma,
         ],
         compiler_params=pltpu.CompilerParams(
             collective_id=0, has_side_effects=True, vmem_limit_bytes=56 * 2**20
@@ -776,25 +755,35 @@
         norm_train[None],
         norm_step[None],
     )
-    ends = (0, chips - 1)
-    out = [
-        (near * CORES + c, end * CORES + c)
-        for near, end in ((1, 0), (chips - 2, chips - 1))
-        for c in range(CORES)
-    ]
-    across = [(end * CORES + c, end * CORES + 1 - c) for end in ends for c in range(CORES)]
+    first = wide - late - span
+    ends = ((1, 0), (chips - 2, chips - 1))
+
+    def send(piece, *pairs):
+        return lax.ppermute(
+            piece,
+            "rows",
+            [
+                (source * CORES + a, target * CORES + b)
+                for near, end in ends
+                for hop in pairs
+                for (source, a), (target, b) in [
+                    ((near if hop[0] else end, hop[1]), (end, hop[2]))
+                ]
+            ],
+        )
 
     def last_hop(piece):
-        return lax.ppermute(piece, "rows", out)
+        return send(piece, (True, 0, 0), (True, 1, 1))
 
     def to_side(piece):
-        return lax.ppermute(piece, "rows", across)
-
+        return send(piece, (False, 0, 1), (False, 1, 0))
+
+    got_early = send(far_early, (True, 0, 0))
     got_query = last_hop(far_query)
     got_key = last_hop(far_key)
     got_value = last_hop(far_value)
     new_query, new_value, scale_key, scale_value, done = settled(
-        query, value, scale_key, scale_value, wide - late
+        query, value, scale_key, scale_value, first
     )
     small = (
         scale_query[0],
@@ -802,12 +791,17 @@
         scale_value[0],
         norms.transpose(1, 0, 2, 3).reshape(-1).astype(jnp.bfloat16),
     )
-    got_query, done = lax.optimization_barrier((got_query, done))
+    got_early, far_early, done = lax.optimization_barrier((got_early, far_early, done))
+    sides = send(far_early, (False, 1, 0)), send(got_early, (False, 0, 1))
     new_query = blended(
-        ranks, wide - late, new_query, query, got_query, to_side(got_query), done
+        ranks, first, new_query, query, (got_early, far_early), sides, done
+    )
+    got_query, new_query = lax.optimization_barrier((got_query, new_query))
+    new_query = blended(
+        ranks, first + span, new_query, query, [got_query] * 2, [to_side(got_query)] * 2, done
     )
     got_key, new_query = lax.optimization_barrier((got_key, new_query))
-    new_key = blended(ranks, 0, done, key, got_key, to_side(got_key), done)
+    new_key = blended(ranks, 0, done, key, [got_key] * 2, [to_side(got_key)] * 2, done)
     got_value, new_key, small = lax.optimization_barrier((got_value, new_key, small))
     new_value = placed(ranks, new_value, got_value, to_side(got_value))
     return (new_query, new_key, new_value, *small)

time: 578 us -> 569 us (0.984)
  Pallas kernels: 525 us -> 508 us
  starting transfers between devices: 9.6 us -> 20.3 us
    pallas_call x1, Pallas kernels: 472 us -> 454 us  [shards(): pl.pallas_call(functools.partial(merge, ranks, widths), out_shape=(shape(...]
    ppermute x6 -> x9, starting transfers between devices: 9.6 us -> 20.3 us  [send(): lax.ppermute(piece, 'rows', [(source * CORES + a, target * CORES + b) for...]
    pallas_call x2 -> x3, Pallas kernels: 17.5 us -> 24.1 us  [blended(): pl.pallas_call(functools.partial(blend_kernel, ranks, first), out_shape=j...]
    pallas_call x1, Pallas kernels: 34.5 us -> 28.4 us  [settled(): pl.pallas_call(settle_kernel, out_shape=(jax.ShapeDtypeStruct(query.shape...]
    ppermute x6 -> x9, waiting for transfers between devices: 37.2 us -> 35.4 us  [send(): lax.ppermute(piece, 'rows', [(source * CORES + a, target * CORES + b) for...]
  transfers between devices with their start and end apart: 6 -> 9, of which waited for: 5 -> 7; matrix products, arithmetic and copies ran while one was open for 0% -> 0% of each run, Pallas kernels for 9% -> 9%
where the time goes in v2:
time: 569 us
  Pallas kernels  508 us (89%)
  waiting for transfers between devices  35.4 us (6%)
  starting transfers between devices  20.3 us (4%)
    pallas_call x1, Pallas kernels, shards(): pl.pallas_call(functools.partial(merge, ranks, widths), out_shape=(shape(...  454 us
    ppermute x9, waiting for transfers between devices, send(): lax.ppermute(piece, 'rows', [(source * CORES + a, target * CORES + b) for...  35.4 us
    pallas_call x1, Pallas kernels, settled(): pl.pallas_call(settle_kernel, out_shape=(jax.ShapeDtypeStruct(query.shape...  28.4 us
    pallas_call x3, Pallas kernels, blended(): pl.pallas_call(functools.partial(blend_kernel, ranks, first), out_shape=j...  24.1 us
    ppermute x9, starting transfers between devices, send(): lax.ppermute(piece, 'rows', [(source * CORES + a, target * CORES + b) for...  20.3 us
  transfers between devices with their start and end apart: 9, of which 7 were waited for; matrix products, arithmetic and copies ran while one was open for 0% of the time, Pallas kernels for 9%

profile of v2, /device:TPU:0, one launch (start us, length us, event | category | flops | bytes accessed | tf_op | source)
XLA Modules:
  0.0 568.6 jit_solution(8426624574323122824)
XLA Ops:
  0.6 453.7 %shard_map.144 = (bf16[7168,3584]{1,0:T(8,128)(2,1)}, bf16[7168,512]{1,0:T(8,128)(2,1)}, bf16[7168,512]{1,0:T(8,128)(2,1)}, bf16[896,512]{1,0:T(8,128)(2,1)}, bf...) custom-call(f32[896,3584]{1,0:T(8,128)} %one_query.1, ...), custom_call_target="tpu_custom_call" | custom-call | tf_op jit(solution)/shard_map/pallas_call | solution.py:697
  454.4 1.3 collective-permute-start.2
  455.7 1.3 collective-permute-start.1
  457.0 0.0 copy-start.3
  457.0 28.4 %shard_map.145 = (bf16[7168,3584]{1,0:T(8,128)(2,1)}, bf16[7168,512]{1,0:T(8,128)(2,1)}, f32[1,512]{1,0:T(1,128)}, f32[1,512]{1,0:T(1,128)}, f32[8,128]{1,0:T(8,128)}) custom-call(bf16[7168,3584]{1,0:T(8,128)(2,1)} %get-tuple-element.38.query.whole, bf16[7168,512]{1,0:T(8,128)(2,1)} %get-tuple-element.39.value, f32[1,512]{1,0:T(1,128)} %get-tuple-element.40.scale_key, ...), custom_call_target="tpu_custom_call" | custom-call | bytes 73400320 | tf_op jit(solution)/shard_map/pallas_call | solution.py:546
  485.4 0.0 collective-permute-done.2.got0
  485.4 0.0 copy-start.4
  485.4 8.0 %collective-permute-start.4 = (bf16[896,512]{1,0:T(8,128)(2,1)S(1)}, bf16[896,512]{1,0:T(8,128)(2,1)S(1)}, u32[]{:S(2)}, u32[]{:S(2)}) collective-permute-start(bf16[896,512]{1,0:T(8,128)(2,1)S(1)} %collective-permute-done.2.got0), channel_id=1, source_target_pairs={{0,2},{12,14},{1,3},{13,15},{16,18},{28,30},{17,19},{29,31}} | collective-permute-start | bytes 2752520 | tf_op jit(solution)/shard_map/ppermute | solution.py:762
  493.5 0.0 copy-done.3
  493.5 1.3 collective-permute-start.3
  494.8 0.7 collective-permute-done.4.side1
  495.5 0.0 copy-start.5
  495.5 2.4 collective-permute-done.3.side0
  497.9 0.0 copy-done.5
  497.9 0.0 copy-start.6
  497.9 0.9 copy-done.6
  498.8 0.0 copy-done.4
  498.8 6.7 %shard_map.146.fresh = bf16[7168,3584]{1,0:T(8,128)(2,1)} custom-call(bf16[7168,3584]{1,0:T(8,128)(2,1)} %get-tuple-element.42.fresh, bf16[7168,3584]{1,0:T(8,128)(2,1)} %get-tuple-element.38.query.whole, bf16[896,512]{1,0:T(8,128)(2,1)} %copy-done.4, bf16[896,512]{1,0:T(8,128)(2,1)} %get-tuple-element.46.got1, ...), custom_call_target="tpu_custom_call", output_to_operand_aliasing={{}: (0, {})} | custom-call | bytes 14680064 | tf_op jit(solution)/shard_map/pallas_call | solution.py:616
  505.5 3.7 collective-permute-done.1.got0.got1
  509.2 0.0 copy-start
  509.2 1.9 collective-permute-start.5
  511.1 0.0 copy-start.7
  511.1 0.0 copy-start.8
  511.2 1.4 collective-permute-start
  512.6 2.3 collective-permute-done.5.side0.side1
  514.9 0.0 copy-done
  514.9 0.0 copy-start.1
  514.9 1.3 copy-done.1
  516.1 10.8 %shard_map.147 = bf16[7168,3584]{1,0:T(8,128)(2,1)} custom-call(bf16[7168,3584]{1,0:T(8,128)(2,1)} %shard_map.146.fresh, bf16[7168,3584]{1,0:T(8,128)(2,1)} %get-tuple-element.38.query.whole, bf16[896,1024]{1,0:T(8,128)(2,1)} %copy-done, bf16[896,1024]{1,0:T(8,128)(2,1)} %copy-done, bf16[896,1024]{1,0:T(8,128)(2,1)} %copy-done.1, ...), custom_call_target="tpu_custom_call", output_to_operand_aliasing={{}: (0, {})} | custom-call | bytes 29360128 | tf_op jit(solution)/shard_map/pallas_call | solution.py:616
  526.9 9.3 %collective-permute-done.got0.got1 = bf16[896,512]{1,0:T(8,128)(2,1)} collective-permute-done((bf16[896,512]{1,0:T(8,128)(2,1)}, bf16[896,512]{1,0:T(8,128)(2,1)}, u32[]{:S(2)}, u32[]{:S(2)}) %collective-permute-start) | collective-permute-done | bytes 917536 | tf_op jit(solution)/shard_map/ppermute | solution.py:762
  536.2 1.9 collective-permute-start.7
  538.2 1.3 collective-permute-start.6
  539.5 0.0 copy-done.7
  539.5 0.7 convert_element_type.11
  540.2 0.0 copy-done.8
  540.2 0.6 reduce
  540.9 0.0 collective-permute-done.7.side0.side1
  540.9 0.0 copy-start.2
  540.9 0.9 copy-done.2
  541.8 6.7 %shard_map.148 = bf16[7168,512]{1,0:T(8,128)(2,1)} custom-call(f32[8,128]{1,0:T(8,128)} %get-tuple-element.47.done.fresh, bf16[7168,512]{1,0:T(8,128)(2,1)} %get-tuple-element.52.whole, bf16[896,512]{1,0:T(8,128)(2,1)} %collective-permute-done.got0.got1, bf16[896,512]{1,0:T(8,128)(2,1)} %collective-permute-done.got0.got1, bf16[896,512]{1,0:T(8,128)(2,1)} %copy-done.2, ...), custom_call_target="tpu_custom_call" | custom-call | bytes 14680064 | tf_op jit(solution)/shard_map/pallas_call | solution.py:616
  548.5 14.5 %collective-permute-done.6.got = bf16[896,512]{1,0:T(8,128)(2,1)S(1)} collective-permute-done((bf16[896,512]{1,0:T(8,128)(2,1)}, bf16[896,512]{1,0:T(8,128)(2,1)S(1)}, u32[]{:S(2)}, u32[]{:S(2)}) %collective-permute-start.6) | collective-permute-done | bytes 917536 | tf_op jit(solution)/shard_map/ppermute | solution.py:762
  563.0 1.9 collective-permute-start.8
  564.9 2.4 collective-permute-done.8.side
  567.4 1.2 shard_map.149
  (2 shorter events, 0.1 us)
Async XLA Ops:
  454.4 31.0 %collective-permute-start.2 = (bf16[896,512]{1,0:T(8,128)(2,1)}, bf16[896,512]{1,0:T(8,128)(2,1)S(1)}, u32[]{:S(2)}, u32[]{:S(2)}) collective-permute-start(bf16[896,512]{1,0:T(8,128)(2,1)} %get-tuple-element.46.got1), channel_id=1, source_target_pairs={{4,0},{8,12},{5,1},{9,13},{20,16},{24,28},{21,17},{25,29}} | collective-permute-start | bytes 2752520 | tf_op jit(solution)/shard_map/ppermute | solution.py:762
  455.7 53.5 %collective-permute-start.1 = (bf16[896,1024]{1,0:T(8,128)(2,1)}, bf16[896,1024]{1,0:T(8,128)(2,1)S(1)}, u32[]{:S(2)}, u32[]{:S(2)}) collective-permute-start(bf16[896,1024]{1,0:T(8,128)(2,1)} %get-tuple-element.37), channel_id=1, source_target_pairs={{4,0},{6,2},{8,12},{10,14},{5,1},{7,3},{9,13},{11,15},{20,16},{22,... | collective-permute-start | bytes 5505032 | tf_op jit(solution)/shard_map/ppermute | solution.py:762
  457.0 36.5 %copy-start.3 = (bf16[896,512]{1,0:T(8,128)(2,1)S(1)}, bf16[896,512]{1,0:T(8,128)(2,1)}, u32[]{:S(2)}) copy-start(bf16[896,512]{1,0:T(8,128)(2,1)} %get-tuple-element.46.got1) | copy-start | bytes 2752516
  485.4 13.4 %copy-start.4 = (bf16[896,512]{1,0:T(8,128)(2,1)}, bf16[896,512]{1,0:T(8,128)(2,1)S(1)}, u32[]{:S(2)}) copy-start(bf16[896,512]{1,0:T(8,128)(2,1)S(1)} %collective-permute-done.2.got0) | copy-start | bytes 2752516
  485.4 10.1 %collective-permute-start.4 = (bf16[896,512]{1,0:T(8,128)(2,1)S(1)}, bf16[896,512]{1,0:T(8,128)(2,1)S(1)}, u32[]{:S(2)}, u32[]{:S(2)}) collective-permute-start(bf16[896,512]{1,0:T(8,128)(2,1)S(1)} %collective-permute-done.2.got0), channel_id=1, source_target_pairs={{0,2},{12,14},{1,3},{13,15},{16,18},{28,30},{17,19},{29,31}} | collective-permute-start | bytes 2752520 | tf_op jit(solution)/shard_map/ppermute | solution.py:762
  493.5 4.4 collective-permute-start.3
  495.5 2.4 copy-start.5
  497.9 0.9 copy-start.6
  509.2 5.7 copy-start
  509.2 5.7 collective-permute-start.5
  511.1 28.3 %copy-start.7 = (f32[2,8,1,448]{3,2,1,0:T(1,128)S(1)}, f32[2,8,1,448]{3,2,1,0:T(1,128)}, u32[]{:S(2)}) copy-start(f32[2,8,1,448]{3,2,1,0:T(1,128)} %get-tuple-element.57) | copy-start | bytes 86020
  511.1 29.1 %copy-start.8 = (f32[1,3584]{1,0:T(1,128)S(1)}, f32[1,3584]{1,0:T(1,128)}, u32[]{:S(2)}) copy-start(f32[1,3584]{1,0:T(1,128)} %get-tuple-element.54) | copy-start | bytes 43012
  511.2 25.1 %collective-permute-start = (bf16[896,512]{1,0:T(8,128)(2,1)}, bf16[896,512]{1,0:T(8,128)(2,1)}, u32[]{:S(2)}, u32[]{:S(2)}) collective-permute-start(bf16[896,512]{1,0:T(8,128)(2,1)} %get-tuple-element.36), channel_id=1, source_target_pairs={{4,0},{6,2},{8,12},{10,14},{5,1},{7,3},{9,13},{11,15},{20,16},{22,... | collective-permute-start | bytes 2752520 | tf_op jit(solution)/shard_map/ppermute | solution.py:762
  514.9 1.3 copy-start.1
  536.2 4.6 collective-permute-start.7
  538.2 24.9 %collective-permute-start.6 = (bf16[896,512]{1,0:T(8,128)(2,1)}, bf16[896,512]{1,0:T(8,128)(2,1)S(1)}, u32[]{:S(2)}, u32[]{:S(2)}) collective-permute-start(bf16[896,512]{1,0:T(8,128)(2,1)} %get-tuple-element.51), channel_id=1, source_target_pairs={{4,0},{6,2},{8,12},{10,14},{5,1},{7,3},{9,13},{11,15},{20,16},{22,... | collective-permute-start | bytes 2752520 | tf_op jit(solution)/shard_map/ppermute | solution.py:762
  540.9 0.9 copy-start.2
  563.0 4.4 collective-permute-start.8

commit v3 on v2

--- a/solution.py
+++ b/solution.py
@@ -13,6 +13,7 @@
 LANES = 128
 LATE = 2
 AHEAD = 3
+HEAD = 160
 
 
 def merge(
@@ -34,6 +35,7 @@
     far_query,
     far_key,
     far_value,
+    far_rest,
     scale_query,
     scale_key,
     scale_value,
@@ -47,6 +49,8 @@
     norms,
     scales,
     peaks,
+    head,
+    narrow_head,
     small_sem,
     load_sem,
     out_sem,
@@ -66,6 +70,9 @@
     side_recv,
     early_send,
     early_recv,
+    head_send,
+    head_recv,
+    head_out,
 ):
     depth, span = one_key.shape
     parts = one_query.shape[1] // span
@@ -78,6 +85,8 @@
     last = early - 1
     block = 32 if depth % 32 == 0 else depth
     late_parts = range(early, parts + 2)
+    taken = head.shape[0]
+    rest = pl.ds(taken, depth - taken)
 
     def is_static(k):
         return isinstance(k, int)
@@ -179,29 +188,32 @@
             return (key if k == parts else value).at[rows]
         return query.at[rows, pl.ds(pl.multiple_of(k * span, span), span)]
 
-    def send(k, rank, to, send_sem, recv_sem, source=None):
+    def send(k, rank, to, send_sem, recv_sem, source=None, cut=None):
+        target = slot(k, rank)
+        source = target if source is None else source
+        if cut is not None:
+            source, target = source.at[cut], target.at[cut]
         return pltpu.make_async_remote_copy(
-            src_ref=slot(k, rank) if source is None else source,
-            dst_ref=slot(k, rank),
+            src_ref=source,
+            dst_ref=target,
             send_sem=send_sem,
             recv_sem=recv_sem,
             device_id={"rows": to},
             device_id_type=MESH,
         )
 
-    def go_up(k, hop, source=None):
-        return send(k, me - CORES * hop, me + CORES, up_send.at[hop, k], up_recv.at[hop, k], source)
-
-    def go_down(k, hop, source=None):
-        return send(
-            k, me + CORES * hop, me - CORES, down_send.at[hop, k], down_recv.at[hop, k], source
-        )
-
-    def go_side(k, hop, source=None):
+    def go_up(k, hop, source=None, cut=None):
+        sems = up_send.at[hop, k], up_recv.at[hop, k]
+        return send(k, me - CORES * hop, me + CORES, *sems, source, cut)
+
+    def go_down(k, hop, source=None, cut=None):
+        sems = down_send.at[hop, k], down_recv.at[hop, k]
+        return send(k, me + CORES * hop, me - CORES, *sems, source, cut)
+
+    def go_side(k, hop, source=None, cut=None):
         index = hop + chips - 1
-        return send(
-            k, me + CORES * hop, partner, side_send.at[index, k], side_recv.at[index, k], source
-        )
+        sems = side_send.at[index, k], side_recv.at[index, k]
+        return send(k, me + CORES * hop, partner, *sems, source, cut)
 
     def from_side(k, hop):
         index = hop + chips - 1
@@ -209,13 +221,21 @@
             k, partner + CORES * hop, partner, side_send.at[index, k], side_recv.at[index, k]
         )
 
-    def from_below(k, hop):
-        return send(k, me - CORES * (hop + 1), me - CORES, up_send.at[hop, k], up_recv.at[hop, k])
-
-    def from_above(k, hop):
-        return send(
-            k, me + CORES * (hop + 1), me + CORES, down_send.at[hop, k], down_recv.at[hop, k]
-        )
+    def from_below(k, hop, cut=None):
+        sems = up_send.at[hop, k], up_recv.at[hop, k]
+        return send(k, me - CORES * (hop + 1), me - CORES, *sems, None, cut)
+
+    def from_above(k, hop, cut=None):
+        sems = down_send.at[hop, k], down_recv.at[hop, k]
+        return send(k, me + CORES * (hop + 1), me + CORES, *sems, None, cut)
+
+    def whole_or_rest(k, headed, action):
+        if is_static(k):
+            action(None)
+            return
+        headed = headed & (k == 0)
+        pl.when(headed)(lambda: action(rest))
+        pl.when(jnp.logical_not(headed))(lambda: action(None))
 
     has_below, has_above = chip >= 1, chip < chips - 1
 
@@ -244,11 +264,11 @@
 
         @pl.when(has_below)
         def _():
-            go_down(k, 0, source).start()
+            whole_or_rest(k, chip == 1, lambda cut: go_down(k, 0, source, cut).start())
 
         @pl.when(has_above)
         def _():
-            go_up(k, 0, source).start()
+            whole_or_rest(k, chip == chips - 2, lambda cut: go_up(k, 0, source, cut).start())
 
         go_side(k, 0, source).start()
         keep(k).start()
@@ -259,14 +279,57 @@
     pl.semaphore_wait(barrier, ranks + widths - 2)
     pl.loop(0, lag)(send_peaks)
 
+    def send_head(to):
+        return pltpu.make_async_remote_copy(
+            src_ref=one.at[0, pl.ds(0, taken)],
+            dst_ref=head,
+            send_sem=head_send,
+            recv_sem=head_recv,
+            device_id={"rows": to},
+            device_id_type=MESH,
+        )
+
+    near_end = (chip == 1) | (chip == chips - 2)
+    at_end = (chip == 0) | (chip == chips - 1)
+    near_rank = jnp.where(chip == 0, me + CORES, me - CORES)
+
+    @pl.when(near_end)
+    def _():
+        send_head(jnp.where(chip == 1, me - CORES, me + CORES)).start()
+
     def advance(k):
         mixed(k)
         send_peaks(k)
 
-    @pl.loop(0, parts - lag)
+    ahead = min(lag + 1, parts)
+    pl.loop(lag, ahead)(advance)
+
+    def head_slot():
+        return slot(jnp.int32(0), near_rank).at[pl.ds(0, taken)]
+
+    def keep_head():
+        return pltpu.make_async_copy(narrow_head, head_slot(), head_out)
+
+    @pl.loop(0, parts - ahead)
     def _(k):
         scaled(k)
-        advance(k + lag)
+        advance(k + ahead)
+
+        @pl.when(at_end & (k == 0))
+        def _():
+            send_head(near_rank).wait_recv()
+            narrow_head[...] = (head[...] / scales[0]).astype(jnp.bfloat16)
+            keep_head().start()
+            hop = jnp.where(chip == 0, 1, -1)
+            index = hop + chips - 1
+            pltpu.make_async_remote_copy(
+                src_ref=narrow_head,
+                dst_ref=head_slot(),
+                send_sem=side_send.at[index, 0],
+                recv_sem=side_recv.at[index, 0],
+                device_id={"rows": partner},
+                device_id_type=MESH,
+            ).start()
 
     advance(parts)
     advance(parts + 1)
@@ -282,7 +345,7 @@
             device_id_type=MESH,
         ).start()
 
-    pl.loop(parts - lag, parts)(scaled)
+    pl.loop(parts - ahead, parts)(scaled)
     scaled(parts)
     scaled(parts + 1)
 
@@ -300,14 +363,23 @@
             device_id_type=MESH,
         ).start()
 
-    def far_copy(k, rank):
-        if is_tail(k):
-            target = far_key if k == parts else far_value
-        elif k == last:
-            target = far_early
-        else:
-            target = far_query.at[:, pl.ds((k - early) * span, span)]
-        return pltpu.make_async_copy(slot(k, rank), target, far_sem.at[k - last])
+    def far_copies(k, rank):
+        source, at = slot(k, rank), far_sem.at[k - last]
+        if k <= parts:
+            if k == last:
+                target = far_early
+            elif k == parts:
+                target = far_key
+            else:
+                target = far_query.at[:, pl.ds((k - early) * span, span)]
+            return [pltpu.make_async_copy(source, target, at)]
+        most = far_value.shape[0]
+        return [
+            pltpu.make_async_copy(source.at[pl.ds(0, most)], far_value, at),
+            pltpu.make_async_copy(
+                source.at[pl.ds(most, depth - most)], far_rest, far_sem.at[k - last + 1]
+            ),
+        ]
 
     def last_early(rank, to):
         return pltpu.make_async_remote_copy(
@@ -326,13 +398,14 @@
 
         @pl.when(chip >= hop)
         def _():
-            from_below(k, hop - 1).wait_recv()
+            headed = (chip == chips - 1) & (hop == 1)
+            whole_or_rest(k, headed, lambda cut: from_below(k, hop - 1, cut).wait_recv())
 
             @pl.when(has_above & onward)
             def _():
                 go_up(k, hop).start()
 
-            go_side(k, -hop).start()
+            whole_or_rest(k, headed, lambda cut: go_side(k, -hop, None, cut).start())
 
             if is_last:
 
@@ -344,17 +417,19 @@
 
                 @pl.when((hop == chips - 2) & (chip == chips - 2))
                 def _():
-                    far_copy(k, me - CORES * hop).start()
+                    for copy in far_copies(k, me - CORES * hop):
+                        copy.start()
 
         @pl.when(chip + hop < chips)
         def _():
-            from_above(k, hop - 1).wait_recv()
+            headed = (chip == 0) & (hop == 1)
+            whole_or_rest(k, headed, lambda cut: from_above(k, hop - 1, cut).wait_recv())
 
             @pl.when(has_below & onward)
             def _():
                 go_down(k, hop).start()
 
-            go_side(k, hop).start()
+            whole_or_rest(k, headed, lambda cut: go_side(k, hop, None, cut).start())
 
             if is_last:
 
@@ -366,7 +441,8 @@
 
                 @pl.when((hop == chips - 2) & (chip == 1))
                 def _():
-                    far_copy(k, me + CORES * hop).start()
+                    for copy in far_copies(k, me + CORES * hop):
+                        copy.start()
 
     @pl.loop(1, chips - 1)
     def _(hop):
@@ -384,11 +460,13 @@
         def _(hop):
             @pl.when((chip >= hop) & has_above)
             def _():
-                go_up(k, hop).wait_send()
+                headed = (chip == chips - 2) & (hop == 0)
+                whole_or_rest(k, headed, lambda cut: go_up(k, hop, None, cut).wait_send())
 
             @pl.when((chip + hop < chips) & has_below)
             def _():
-                go_down(k, hop).wait_send()
+                headed = (chip == 1) & (hop == 0)
+                whole_or_rest(k, headed, lambda cut: go_down(k, hop, None, cut).wait_send())
 
         @pl.loop(0, chips)
         def _(origin):
@@ -401,15 +479,21 @@
         everyone = peaks.at[k, pl.ds(0, ranks - 1)]
         pltpu.make_async_copy(everyone, everyone, peak_send.at[k]).wait()
 
-    near_end = (chip == 1) | (chip == chips - 2)
-    at_end = (chip == 0) | (chip == chips - 1)
-
     for k in (last, *late_parts):
         finish(k)
 
         @pl.when(near_end)
         def _():
-            far_copy(k, me).wait()
+            for copy in far_copies(k, me):
+                copy.wait()
+
+    @pl.when(near_end)
+    def _():
+        send_head(partner).wait_send()
+
+    @pl.when(at_end)
+    def _():
+        keep_head().wait()
 
     pl.loop(0, parts + 2)(settle)
     pltpu.make_async_copy(others, others, norm_send).wait()
@@ -630,39 +714,42 @@
     )(fresh, whole, *gots, *sides, done)
 
 
-def place_kernel(ranks, _, got, side, target, sems):
+def place_kernel(ranks, depth, _, *refs):
+    gots, sides, (target, sems) = refs[0:2], refs[2:4], refs[4:]
     at_end, straight, crossed = far_ranks(ranks)
-    depth = got.shape[0]
 
     @pl.when(at_end)
     def _():
-        copies = [
-            pltpu.make_async_copy(
-                source, target.at[pl.ds(pl.multiple_of(rank * depth, depth), depth)], sems.at[i]
-            )
-            for i, (source, rank) in enumerate(((got, straight), (side, crossed)))
-        ]
+        copies = []
+        for rank, pieces in ((straight, gots), (crossed, sides)):
+            row = rank * depth
+            for piece in pieces:
+                rows = pl.ds(pl.multiple_of(row, 8), piece.shape[0])
+                at = sems.at[len(copies)]
+                copies.append(pltpu.make_async_copy(piece, target.at[rows], at))
+                row = row + piece.shape[0]
         for copy in copies:
             copy.start()
         for copy in copies:
             copy.wait()
 
 
-def placed(ranks, whole, got, side):
+def placed(ranks, whole, gots, sides):
     anywhere = pl.BlockSpec(memory_space=pl.ANY)
     near = pl.BlockSpec(memory_space=pltpu.VMEM)
+    depth = whole.shape[0] // ranks
     return pl.pallas_call(
-        functools.partial(place_kernel, ranks),
+        functools.partial(place_kernel, ranks, depth),
         out_shape=jax.ShapeDtypeStruct(whole.shape, whole.dtype),
-        in_specs=[anywhere, near, near],
+        in_specs=[anywhere, near, near, near, near],
         out_specs=anywhere,
-        scratch_shapes=[pltpu.SemaphoreType.DMA((2,))],
+        scratch_shapes=[pltpu.SemaphoreType.DMA((4,))],
         input_output_aliases={0: 0},
         compiler_params=pltpu.CompilerParams(vmem_limit_bytes=8 * 2**20),
         cost_estimate=pl.CostEstimate(
-            flops=0, bytes_accessed=4 * got.size, transcendentals=0
+            flops=0, bytes_accessed=8 * gots[0].size, transcendentals=0
         ),
-    )(whole, got, side)
+    )(whole, *gots, *sides)
 
 
 def shards(
@@ -684,6 +771,8 @@
     chips = ranks // CORES
     bit = norm_train.shape[0]
     late = LATE * span
+    tail = max(8, depth // 64 * 8)
+    head = min(HEAD, depth // 16 * 8)
     tall = -(-depth // LANES) * LANES
     if tall != depth:
         mix_share = jnp.pad(mix_share, (0, tall - depth))
@@ -692,7 +781,7 @@
     anywhere = pl.BlockSpec(memory_space=pl.ANY)
     dma = pltpu.SemaphoreType.DMA
     (
-        query, key, value, far_early, far_query, far_key, far_value,
+        query, key, value, far_early, far_query, far_key, far_value, far_rest,
         scale_query, scale_key, scale_value, norms,
     ) = pl.pallas_call(
         functools.partial(merge, ranks, widths),
@@ -703,14 +792,15 @@
             shape((depth, span), jnp.bfloat16),
             shape((depth, late), jnp.bfloat16),
             shape((depth, span), jnp.bfloat16),
-            shape((depth, span), jnp.bfloat16),
+            shape((depth - tail, span), jnp.bfloat16),
+            shape((tail, span), jnp.bfloat16),
             shape((1, wide), jnp.float32),
             shape((1, span), jnp.float32),
             shape((1, span), jnp.float32),
             shape((widths, ranks, 1, bit), jnp.float32),
         ),
         in_specs=[anywhere] * 9,
-        out_specs=[anywhere] * 11,
+        out_specs=[anywhere] * 12,
         scratch_shapes=[
             pltpu.VMEM((parts + 2, depth, span), jnp.float32),
             pltpu.VMEM((parts + 2, depth, span), jnp.float32),
@@ -721,11 +811,13 @@
             pltpu.VMEM((widths, ranks, 1, bit), jnp.float32),
             pltpu.VMEM((parts + 2, 1, span), jnp.float32),
             pltpu.VMEM((parts + 2, ranks, 1, span), jnp.float32),
+            pltpu.VMEM((head, span), jnp.float32),
+            pltpu.VMEM((head, span), jnp.bfloat16),
             dma((4,)),
             dma((2, parts + 2)),
             dma((parts + 2,)),
             dma((parts + 2,)),
-            dma((LATE + 3,)),
+            dma((LATE + 4,)),
             dma((parts + 2,)),
             dma((parts + 2,)),
             dma,
@@ -738,6 +830,9 @@
             dma((chips - 1, parts + 2)),
             dma((2 * chips - 1, parts + 2)),
             dma((2 * chips - 1, parts + 2)),
+            dma,
+            dma,
+            dma,
             dma,
             dma,
         ],
@@ -782,6 +877,7 @@
     got_query = last_hop(far_query)
     got_key = last_hop(far_key)
     got_value = last_hop(far_value)
+    got_rest = last_hop(far_rest)
     new_query, new_value, scale_key, scale_value, done = settled(
         query, value, scale_key, scale_value, first
     )
@@ -803,7 +899,8 @@
     got_key, new_query = lax.optimization_barrier((got_key, new_query))
     new_key = blended(ranks, 0, done, key, [got_key] * 2, [to_side(got_key)] * 2, done)
     got_value, new_key, small = lax.optimization_barrier((got_value, new_key, small))
-    new_value = placed(ranks, new_value, got_value, to_side(got_value))
+    sides = to_side(got_value), to_side(got_rest)
+    new_value = placed(ranks, new_value, (got_value, got_rest), sides)
     return (new_query, new_key, new_value, *small)
 
 

time: 569 us -> 575 us (1.011)
    ppermute x9 -> x11, starting transfers between devices: 20.3 us -> 23.4 us  [send(): lax.ppermute(piece, 'rows', [(source * CORES + a, target * CORES + b) for...]
    ppermute x9 -> x11, waiting for transfers between devices: 35.4 us -> 37.9 us  [send(): lax.ppermute(piece, 'rows', [(source * CORES + a, target * CORES + b) for...]
  transfers between devices with their start and end apart: 9 -> 11, of which waited for: 7 -> 7; matrix products, arithmetic and copies ran while one was open for 0% -> 0% of each run, Pallas kernels for 9% -> 9%
where the time goes in v3:
time: 575 us; the launch traced here: 574 us
  Pallas kernels  507 us (88%)
  waiting for transfers between devices  37.9 us (7%)
  starting transfers between devices  23.4 us (4%)
    pallas_call x1, Pallas kernels, shards(): pl.pallas_call(functools.partial(merge, ranks, widths), out_shape=(shape(...  454 us
    ppermute x11, waiting for transfers between devices, send(): lax.ppermute(piece, 'rows', [(source * CORES + a, target * CORES + b) for...  37.9 us
    pallas_call x1, Pallas kernels, settled(): pl.pallas_call(settle_kernel, out_shape=(jax.ShapeDtypeStruct(query.shape...  28.4 us
    pallas_call x3, Pallas kernels, blended(): pl.pallas_call(functools.partial(blend_kernel, ranks, first), out_shape=j...  24.2 us
    ppermute x11, starting transfers between devices, send(): lax.ppermute(piece, 'rows', [(source * CORES + a, target * CORES + b) for...  23.4 us
  transfers between devices with their start and end apart: 11, of which 7 were waited for; matrix products, arithmetic and copies ran while one was open for 0% of the time, Pallas kernels for 9%

profile of v3, /device:TPU:0, one launch (start us, length us, event | category | flops | bytes accessed | tf_op | source)
XLA Modules:
  0.0 574.3 jit_solution(8074853038266343783)
XLA Ops:
  0.6 453.6 %shard_map.144 = (bf16[7168,3584]{1,0:T(8,128)(2,1)}, bf16[7168,512]{1,0:T(8,128)(2,1)}, bf16[7168,512]{1,0:T(8,128)(2,1)}, bf16[896,512]{1,0:T(8,128)(2,1)}, bf...) custom-call(f32[896,3584]{1,0:T(8,128)} %one_query.1, ...), custom_call_target="tpu_custom_call" | custom-call | tf_op jit(solution)/shard_map/pallas_call | solution.py:786
  454.3 1.3 collective-permute-start.2
  455.6 1.3 collective-permute-start.1
  456.9 0.0 copy-start.3
  456.9 28.4 %shard_map.145 = (bf16[7168,3584]{1,0:T(8,128)(2,1)}, bf16[7168,512]{1,0:T(8,128)(2,1)}, f32[1,512]{1,0:T(1,128)}, f32[1,512]{1,0:T(1,128)}, f32[8,128]{1,0:T(8,128)}) custom-call(bf16[7168,3584]{1,0:T(8,128)(2,1)} %get-tuple-element.39.query.whole, bf16[7168,512]{1,0:T(8,128)(2,1)} %get-tuple-element.40.value, f32[1,512]{1,0:T(1,128)} %get-tuple-element.41.scale_key, ...), custom_call_target="tpu_custom_call" | custom-call | bytes 73400320 | tf_op jit(solution)/shard_map/pallas_call | solution.py:630
  485.3 0.0 collective-permute-done.2.got0
  485.3 0.0 copy-start.4
  485.3 0.0 copy-done.3
  485.4 1.3 collective-permute-start.3
  486.7 7.9 %collective-permute-start.4 = (bf16[896,512]{1,0:T(8,128)(2,1)S(1)}, bf16[896,512]{1,0:T(8,128)(2,1)S(1)}, u32[]{:S(2)}, u32[]{:S(2)}) collective-permute-start(bf16[896,512]{1,0:T(8,128)(2,1)S(1)} %collective-permute-done.2.got0), channel_id=1, source_target_pairs={{0,2},{12,14},{1,3},{13,15},{16,18},{28,30},{17,19},{29,31}} | collective-permute-start | bytes 2752520 | tf_op jit(solution)/shard_map/ppermute | solution.py:857
  494.5 0.0 collective-permute-done.3.side0
  494.6 0.0 copy-start.5
  494.6 2.0 collective-permute-done.4.side1
  496.6 0.0 copy-done.5
  496.6 0.0 copy-start.6
  496.6 1.0 copy-done.6
  497.6 0.0 copy-done.4
  497.6 6.7 %shard_map.146.fresh = bf16[7168,3584]{1,0:T(8,128)(2,1)} custom-call(bf16[7168,3584]{1,0:T(8,128)(2,1)} %get-tuple-element.43.fresh, bf16[7168,3584]{1,0:T(8,128)(2,1)} %get-tuple-element.39.query.whole, bf16[896,512]{1,0:T(8,128)(2,1)} %copy-done.4, bf16[896,512]{1,0:T(8,128)(2,1)} %get-tuple-element.47.got1, ...), custom_call_target="tpu_custom_call", output_to_operand_aliasing={{}: (0, {})} | custom-call | bytes 14680064 | tf_op jit(solution)/shard_map/pallas_call | solution.py:700
  504.3 4.8 collective-permute-done.1.got0.got1
  509.1 0.0 copy-start
  509.1 1.9 collective-permute-start.5
  511.0 0.0 copy-start.7
  511.0 0.0 copy-start.8
  511.0 1.4 collective-permute-start
  512.5 2.3 collective-permute-done.5.side0.side1
  514.8 0.0 copy-done
  514.8 0.0 copy-start.1
  514.8 1.3 copy-done.1
  516.0 10.8 %shard_map.147 = bf16[7168,3584]{1,0:T(8,128)(2,1)} custom-call(bf16[7168,3584]{1,0:T(8,128)(2,1)} %shard_map.146.fresh, bf16[7168,3584]{1,0:T(8,128)(2,1)} %get-tuple-element.39.query.whole, bf16[896,1024]{1,0:T(8,128)(2,1)} %copy-done, bf16[896,1024]{1,0:T(8,128)(2,1)} %copy-done, bf16[896,1024]{1,0:T(8,128)(2,1)} %copy-done.1, ...), custom_call_target="tpu_custom_call", output_to_operand_aliasing={{}: (0, {})} | custom-call | bytes 29360128 | tf_op jit(solution)/shard_map/pallas_call | solution.py:700
  526.8 9.3 %collective-permute-done.got0.got1 = bf16[896,512]{1,0:T(8,128)(2,1)} collective-permute-done((bf16[896,512]{1,0:T(8,128)(2,1)}, bf16[896,512]{1,0:T(8,128)(2,1)}, u32[]{:S(2)}, u32[]{:S(2)}) %collective-permute-start) | collective-permute-done | bytes 917536 | tf_op jit(solution)/shard_map/ppermute | solution.py:857
  536.1 1.9 collective-permute-start.7
  538.1 1.3 collective-permute-start.6
  539.4 0.0 copy-done.7
  539.4 0.7 convert_element_type.11
  540.1 0.0 copy-done.8
  540.1 0.6 reduce
  540.8 0.0 collective-permute-done.7.side0.side1
  540.8 0.0 copy-start.2
  540.8 0.9 copy-done.2
  541.7 0.0 copy-start.9
  541.7 6.7 %shard_map.148 = bf16[7168,512]{1,0:T(8,128)(2,1)} custom-call(f32[8,128]{1,0:T(8,128)} %get-tuple-element.48.done.fresh, bf16[7168,512]{1,0:T(8,128)(2,1)} %get-tuple-element.53.whole, bf16[896,512]{1,0:T(8,128)(2,1)} %collective-permute-done.got0.got1, bf16[896,512]{1,0:T(8,128)(2,1)} %collective-permute-done.got0.got1, bf16[896,512]{1,0:T(8,128)(2,1)} %copy-done.2, ...), custom_call_target="tpu_custom_call" | custom-call | bytes 14680064 | tf_op jit(solution)/shard_map/pallas_call | solution.py:700
  548.4 12.0 %collective-permute-done.6.refs_0_ = bf16[784,512]{1,0:T(8,128)(2,1)S(1)} collective-permute-done((bf16[784,512]{1,0:T(8,128)(2,1)}, bf16[784,512]{1,0:T(8,128)(2,1)S(1)}, u32[]{:S(2)}, u32[]{:S(2)}) %collective-permute-start.6) | collective-permute-done | bytes 802848 | tf_op jit(solution)/shard_map/ppermute | solution.py:857
  560.5 1.9 collective-permute-start.9
  562.4 0.0 copy-done.9
  562.4 1.3 collective-permute-start.8
  563.7 6.1 %collective-permute-done.8.refs_1_ = bf16[112,512]{1,0:T(8,128)(2,1)S(1)} collective-permute-done((bf16[112,512]{1,0:T(8,128)(2,1)S(1)}, bf16[112,512]{1,0:T(8,128)(2,1)S(1)}, u32[]{:S(2)}, u32[]{:S(2)}) %collective-permute-start.8) | collective-permute-done | bytes 114720 | tf_op jit(solution)/shard_map/ppermute | solution.py:857
  569.8 1.9 collective-permute-start.10
  571.7 1.3 collective-permute-done.10.refs_3_
  573.0 0.0 collective-permute-done.9.refs_2_
  573.0 1.2 shard_map.149
  (2 shorter events, 0.1 us)
Async XLA Ops:
  454.3 31.0 %collective-permute-start.2 = (bf16[896,512]{1,0:T(8,128)(2,1)}, bf16[896,512]{1,0:T(8,128)(2,1)S(1)}, u32[]{:S(2)}, u32[]{:S(2)}) collective-permute-start(bf16[896,512]{1,0:T(8,128)(2,1)} %get-tuple-element.47.got1), channel_id=1, source_target_pairs={{4,0},{8,12},{5,1},{9,13},{20,16},{24,28},{21,17},{25,29}} | collective-permute-start | bytes 2752520 | tf_op jit(solution)/shard_map/ppermute | solution.py:857
  455.6 53.5 %collective-permute-start.1 = (bf16[896,1024]{1,0:T(8,128)(2,1)}, bf16[896,1024]{1,0:T(8,128)(2,1)S(1)}, u32[]{:S(2)}, u32[]{:S(2)}) collective-permute-start(bf16[896,1024]{1,0:T(8,128)(2,1)} %get-tuple-element.38), channel_id=1, source_target_pairs={{4,0},{6,2},{8,12},{10,14},{5,1},{7,3},{9,13},{11,15},{20,16},{22,... | collective-permute-start | bytes 5505032 | tf_op jit(solution)/shard_map/ppermute | solution.py:857
  456.9 28.5 %copy-start.3 = (bf16[896,512]{1,0:T(8,128)(2,1)S(1)}, bf16[896,512]{1,0:T(8,128)(2,1)}, u32[]{:S(2)}) copy-start(bf16[896,512]{1,0:T(8,128)(2,1)} %get-tuple-element.47.got1) | copy-start | bytes 2752516
  485.3 12.2 %copy-start.4 = (bf16[896,512]{1,0:T(8,128)(2,1)}, bf16[896,512]{1,0:T(8,128)(2,1)S(1)}, u32[]{:S(2)}) copy-start(bf16[896,512]{1,0:T(8,128)(2,1)S(1)} %collective-permute-done.2.got0) | copy-start | bytes 2752516
  485.4 9.2 %collective-permute-start.3 = (bf16[896,512]{1,0:T(8,128)(2,1)S(1)}, bf16[896,512]{1,0:T(8,128)(2,1)S(1)}, u32[]{:S(2)}, u32[]{:S(2)}) collective-permute-start(bf16[896,512]{1,0:T(8,128)(2,1)S(1)} %copy-done.3), channel_id=1, source_target_pairs={{2,0},{14,12},{3,1},{15,13},{18,16},{30,28},{19,17},{31,29}} | collective-permute-start | bytes 2752520 | tf_op jit(solution)/shard_map/ppermute | solution.py:857
  486.7 9.9 %collective-permute-start.4 = (bf16[896,512]{1,0:T(8,128)(2,1)S(1)}, bf16[896,512]{1,0:T(8,128)(2,1)S(1)}, u32[]{:S(2)}, u32[]{:S(2)}) collective-permute-start(bf16[896,512]{1,0:T(8,128)(2,1)S(1)} %collective-permute-done.2.got0), channel_id=1, source_target_pairs={{0,2},{12,14},{1,3},{13,15},{16,18},{28,30},{17,19},{29,31}} | collective-permute-start | bytes 2752520 | tf_op jit(solution)/shard_map/ppermute | solution.py:857
  494.6 2.0 copy-start.5
  496.6 1.0 copy-start.6
  509.1 5.7 copy-start
  509.1 5.7 collective-permute-start.5
  511.0 28.3 %copy-start.7 = (f32[2,8,1,448]{3,2,1,0:T(1,128)S(1)}, f32[2,8,1,448]{3,2,1,0:T(1,128)}, u32[]{:S(2)}) copy-start(f32[2,8,1,448]{3,2,1,0:T(1,128)} %get-tuple-element.58) | copy-start | bytes 86020
  511.0 29.1 %copy-start.8 = (f32[1,3584]{1,0:T(1,128)S(1)}, f32[1,3584]{1,0:T(1,128)}, u32[]{:S(2)}) copy-start(f32[1,3584]{1,0:T(1,128)} %get-tuple-element.55) | copy-start | bytes 43012
  511.0 25.1 %collective-permute-start = (bf16[896,512]{1,0:T(8,128)(2,1)}, bf16[896,512]{1,0:T(8,128)(2,1)}, u32[]{:S(2)}, u32[]{:S(2)}) collective-permute-start(bf16[896,512]{1,0:T(8,128)(2,1)} %get-tuple-element.37), channel_id=1, source_target_pairs={{4,0},{6,2},{8,12},{10,14},{5,1},{7,3},{9,13},{11,15},{20,16},{22,... | collective-permute-start | bytes 2752520 | tf_op jit(solution)/shard_map/ppermute | solution.py:857
  514.8 1.3 copy-start.1
  536.1 4.6 collective-permute-start.7
  538.1 22.4 %collective-permute-start.6 = (bf16[784,512]{1,0:T(8,128)(2,1)}, bf16[784,512]{1,0:T(8,128)(2,1)S(1)}, u32[]{:S(2)}, u32[]{:S(2)}) collective-permute-start(bf16[784,512]{1,0:T(8,128)(2,1)} %get-tuple-element.52), channel_id=1, source_target_pairs={{4,0},{6,2},{8,12},{10,14},{5,1},{7,3},{9,13},{11,15},{20,16},{22,... | collective-permute-start | bytes 2408456 | tf_op jit(solution)/shard_map/ppermute | solution.py:857
  540.8 1.0 copy-start.2
  541.7 20.6 %copy-start.9 = (bf16[112,512]{1,0:T(8,128)(2,1)S(1)}, bf16[112,512]{1,0:T(8,128)(2,1)}, u32[]{:S(2)}) copy-start(bf16[112,512]{1,0:T(8,128)(2,1)} %get-tuple-element.62) | copy-start | bytes 344068
  560.5 12.6 %collective-permute-start.9 = (bf16[784,512]{1,0:T(8,128)(2,1)S(1)}, bf16[784,512]{1,0:T(8,128)(2,1)S(1)}, u32[]{:S(2)}, u32[]{:S(2)}) collective-permute-start(bf16[784,512]{1,0:T(8,128)(2,1)S(1)} %collective-permute-done.6.refs_0_), channel_id=1, source_target_pairs={{0,2},{2,0},{12,14},{14,12},{1,3},{3,1},{13,15},{15,13},{16,18},{1... | collective-permute-start | bytes 2408456 | tf_op jit(solution)/shard_map/ppermute | solution.py:857
  562.4 7.4 %collective-permute-start.8 = (bf16[112,512]{1,0:T(8,128)(2,1)S(1)}, bf16[112,512]{1,0:T(8,128)(2,1)S(1)}, u32[]{:S(2)}, u32[]{:S(2)}) collective-permute-start(bf16[112,512]{1,0:T(8,128)(2,1)S(1)} %copy-done.9), channel_id=1, source_target_pairs={{4,0},{6,2},{8,12},{10,14},{5,1},{7,3},{9,13},{11,15},{20,16},{22,... | collective-permute-start | bytes 344072 | tf_op jit(solution)/shard_map/ppermute | solution.py:857
  569.8 3.2 collective-permute-start.10

commit v4 on v3

--- a/solution.py
+++ b/solution.py
@@ -13,7 +13,7 @@
 LANES = 128
 LATE = 2
 AHEAD = 3
-HEAD = 160
+HEAD = 96
 
 
 def merge(
@@ -275,9 +275,9 @@
         keep_scale(k).start()
 
     lag = min(3, parts)
-    pl.loop(0, lag)(mixed)
+    pl.loop(0, 1)(mixed)
     pl.semaphore_wait(barrier, ranks + widths - 2)
-    pl.loop(0, lag)(send_peaks)
+    pl.loop(0, 1)(send_peaks)
 
     def send_head(to):
         return pltpu.make_async_remote_copy(
@@ -301,8 +301,7 @@
         mixed(k)
         send_peaks(k)
 
-    ahead = min(lag + 1, parts)
-    pl.loop(lag, ahead)(advance)
+    pl.loop(1, lag)(advance)
 
     def head_slot():
         return slot(jnp.int32(0), near_rank).at[pl.ds(0, taken)]
@@ -310,10 +309,10 @@
     def keep_head():
         return pltpu.make_async_copy(narrow_head, head_slot(), head_out)
 
-    @pl.loop(0, parts - ahead)
+    @pl.loop(0, parts - lag)
     def _(k):
         scaled(k)
-        advance(k + ahead)
+        advance(k + lag)
 
         @pl.when(at_end & (k == 0))
         def _():
@@ -345,7 +344,7 @@
             device_id_type=MESH,
         ).start()
 
-    pl.loop(parts - ahead, parts)(scaled)
+    pl.loop(parts - lag, parts)(scaled)
     scaled(parts)
     scaled(parts + 1)
 

time: 575 us -> 571 us (level)
  no operation moved by 1% of the time
where the time goes in v4:
time: 571 us; the launch traced here: 570 us
  Pallas kernels  504 us (88%)
  waiting for transfers between devices  37.5 us (7%)
  starting transfers between devices  23.8 us (4%)
    pallas_call x1, Pallas kernels, shards(): pl.pallas_call(functools.partial(merge, ranks, widths), out_shape=(shape(...  450 us
    ppermute x11, waiting for transfers between devices, send(): lax.ppermute(piece, 'rows', [(source * CORES + a, target * CORES + b) for...  37.5 us
    pallas_call x1, Pallas kernels, settled(): pl.pallas_call(settle_kernel, out_shape=(jax.ShapeDtypeStruct(query.shape...  28.4 us
    pallas_call x3, Pallas kernels, blended(): pl.pallas_call(functools.partial(blend_kernel, ranks, first), out_shape=j...  24.2 us
    ppermute x11, starting transfers between devices, send(): lax.ppermute(piece, 'rows', [(source * CORES + a, target * CORES + b) for...  23.8 us
  transfers between devices with their start and end apart: 11, of which 7 were waited for; matrix products, arithmetic and copies ran while one was open for 0% of the time, Pallas kernels for 9%

profile of v4, /device:TPU:0, one launch (start us, length us, event | category | flops | bytes accessed | tf_op | source)
XLA Modules:
  0.0 570.4 jit_solution(9333394957259163439)
XLA Ops:
  0.6 449.7 %shard_map.144 = (bf16[7168,3584]{1,0:T(8,128)(2,1)}, bf16[7168,512]{1,0:T(8,128)(2,1)}, bf16[7168,512]{1,0:T(8,128)(2,1)}, bf16[896,512]{1,0:T(8,128)(2,1)}, bf...) custom-call(f32[896,3584]{1,0:T(8,128)} %one_query.1, ...), custom_call_target="tpu_custom_call" | custom-call | tf_op jit(solution)/shard_map/pallas_call | solution.py:785
  450.4 1.3 collective-permute-start.2
  451.7 1.3 collective-permute-start.1
  453.0 0.0 copy-start.3
  453.0 28.4 %shard_map.145 = (bf16[7168,3584]{1,0:T(8,128)(2,1)}, bf16[7168,512]{1,0:T(8,128)(2,1)}, f32[1,512]{1,0:T(1,128)}, f32[1,512]{1,0:T(1,128)}, f32[8,128]{1,0:T(8,128)}) custom-call(bf16[7168,3584]{1,0:T(8,128)(2,1)} %get-tuple-element.39.query.whole, bf16[7168,512]{1,0:T(8,128)(2,1)} %get-tuple-element.40.value, f32[1,512]{1,0:T(1,128)} %get-tuple-element.41.scale_key, ...), custom_call_target="tpu_custom_call" | custom-call | bytes 73400320 | tf_op jit(solution)/shard_map/pallas_call | solution.py:629
  481.4 0.0 collective-permute-done.2.got0
  481.4 0.0 copy-start.4
  481.4 0.0 copy-done.3
  481.4 1.3 collective-permute-start.3
  482.7 8.3 %collective-permute-start.4 = (bf16[896,512]{1,0:T(8,128)(2,1)S(1)}, bf16[896,512]{1,0:T(8,128)(2,1)S(1)}, u32[]{:S(2)}, u32[]{:S(2)}) collective-permute-start(bf16[896,512]{1,0:T(8,128)(2,1)S(1)} %collective-permute-done.2.got0), channel_id=1, source_target_pairs={{0,2},{12,14},{1,3},{13,15},{16,18},{28,30},{17,19},{29,31}} | collective-permute-start | bytes 2752520 | tf_op jit(solution)/shard_map/ppermute | solution.py:856
  491.0 0.0 collective-permute-done.3.side0
  491.0 0.0 copy-start.5
  491.0 2.0 collective-permute-done.4.side1
  493.0 0.0 copy-done.5
  493.0 0.0 copy-start.6
  493.0 1.0 copy-done.6
  494.0 0.0 copy-done.4
  494.0 6.7 %shard_map.146.fresh = bf16[7168,3584]{1,0:T(8,128)(2,1)} custom-call(bf16[7168,3584]{1,0:T(8,128)(2,1)} %get-tuple-element.43.fresh, bf16[7168,3584]{1,0:T(8,128)(2,1)} %get-tuple-element.39.query.whole, bf16[896,512]{1,0:T(8,128)(2,1)} %copy-done.4, bf16[896,512]{1,0:T(8,128)(2,1)} %get-tuple-element.47.got1, ...), custom_call_target="tpu_custom_call", output_to_operand_aliasing={{}: (0, {})} | custom-call | bytes 14680064 | tf_op jit(solution)/shard_map/pallas_call | solution.py:699
  500.7 4.5 collective-permute-done.1.got0.got1
  505.2 0.0 copy-start
  505.2 1.9 collective-permute-start.5
  507.1 0.0 copy-start.7
  507.1 0.0 copy-start.8
  507.1 1.4 collective-permute-start
  508.6 2.3 collective-permute-done.5.side0.side1
  510.9 0.0 copy-done
  510.9 0.0 copy-start.1
  510.9 1.3 copy-done.1
  512.1 10.8 %shard_map.147 = bf16[7168,3584]{1,0:T(8,128)(2,1)} custom-call(bf16[7168,3584]{1,0:T(8,128)(2,1)} %shard_map.146.fresh, bf16[7168,3584]{1,0:T(8,128)(2,1)} %get-tuple-element.39.query.whole, bf16[896,1024]{1,0:T(8,128)(2,1)} %copy-done, bf16[896,1024]{1,0:T(8,128)(2,1)} %copy-done, bf16[896,1024]{1,0:T(8,128)(2,1)} %copy-done.1, ...), custom_call_target="tpu_custom_call", output_to_operand_aliasing={{}: (0, {})} | custom-call | bytes 29360128 | tf_op jit(solution)/shard_map/pallas_call | solution.py:699
  522.9 9.3 %collective-permute-done.got0.got1 = bf16[896,512]{1,0:T(8,128)(2,1)} collective-permute-done((bf16[896,512]{1,0:T(8,128)(2,1)}, bf16[896,512]{1,0:T(8,128)(2,1)}, u32[]{:S(2)}, u32[]{:S(2)}) %collective-permute-start) | collective-permute-done | bytes 917536 | tf_op jit(solution)/shard_map/ppermute | solution.py:856
  532.2 1.9 collective-permute-start.7
  534.1 1.3 collective-permute-start.6
  535.4 0.0 copy-done.7
  535.5 0.7 convert_element_type.11
  536.2 0.0 copy-done.8
  536.2 0.6 reduce
  536.9 0.0 collective-permute-done.7.side0.side1
  536.9 0.0 copy-start.2
  536.9 0.9 copy-done.2
  537.8 0.0 copy-start.9
  537.8 6.7 %shard_map.148 = bf16[7168,512]{1,0:T(8,128)(2,1)} custom-call(f32[8,128]{1,0:T(8,128)} %get-tuple-element.48.done.fresh, bf16[7168,512]{1,0:T(8,128)(2,1)} %get-tuple-element.53.whole, bf16[896,512]{1,0:T(8,128)(2,1)} %collective-permute-done.got0.got1, bf16[896,512]{1,0:T(8,128)(2,1)} %collective-permute-done.got0.got1, bf16[896,512]{1,0:T(8,128)(2,1)} %copy-done.2, ...), custom_call_target="tpu_custom_call" | custom-call | bytes 14680064 | tf_op jit(solution)/shard_map/pallas_call | solution.py:699
  544.5 12.0 %collective-permute-done.6.refs_0_ = bf16[784,512]{1,0:T(8,128)(2,1)S(1)} collective-permute-done((bf16[784,512]{1,0:T(8,128)(2,1)}, bf16[784,512]{1,0:T(8,128)(2,1)S(1)}, u32[]{:S(2)}, u32[]{:S(2)}) %collective-permute-start.6) | collective-permute-done | bytes 802848 | tf_op jit(solution)/shard_map/ppermute | solution.py:856
  556.5 1.9 collective-permute-start.9
  558.5 0.0 copy-done.9
  558.5 1.3 collective-permute-start.8
  559.8 6.1 %collective-permute-done.8.refs_1_ = bf16[112,512]{1,0:T(8,128)(2,1)S(1)} collective-permute-done((bf16[112,512]{1,0:T(8,128)(2,1)S(1)}, bf16[112,512]{1,0:T(8,128)(2,1)S(1)}, u32[]{:S(2)}, u32[]{:S(2)}) %collective-permute-start.8) | collective-permute-done | bytes 114720 | tf_op jit(solution)/shard_map/ppermute | solution.py:856
  565.9 1.9 collective-permute-start.10
  567.8 1.3 collective-permute-done.10.refs_3_
  569.1 0.0 collective-permute-done.9.refs_2_
  569.1 1.2 shard_map.149
  (2 shorter events, 0.1 us)
Async XLA Ops:
  450.4 31.0 %collective-permute-start.2 = (bf16[896,512]{1,0:T(8,128)(2,1)}, bf16[896,512]{1,0:T(8,128)(2,1)S(1)}, u32[]{:S(2)}, u32[]{:S(2)}) collective-permute-start(bf16[896,512]{1,0:T(8,128)(2,1)} %get-tuple-element.47.got1), channel_id=1, source_target_pairs={{4,0},{8,12},{5,1},{9,13},{20,16},{24,28},{21,17},{25,29}} | collective-permute-start | bytes 2752520 | tf_op jit(solution)/shard_map/ppermute | solution.py:856
  451.7 53.5 %collective-permute-start.1 = (bf16[896,1024]{1,0:T(8,128)(2,1)}, bf16[896,1024]{1,0:T(8,128)(2,1)S(1)}, u32[]{:S(2)}, u32[]{:S(2)}) collective-permute-start(bf16[896,1024]{1,0:T(8,128)(2,1)} %get-tuple-element.38), channel_id=1, source_target_pairs={{4,0},{6,2},{8,12},{10,14},{5,1},{7,3},{9,13},{11,15},{20,16},{22,... | collective-permute-start | bytes 5505032 | tf_op jit(solution)/shard_map/ppermute | solution.py:856
  453.0 28.5 %copy-start.3 = (bf16[896,512]{1,0:T(8,128)(2,1)S(1)}, bf16[896,512]{1,0:T(8,128)(2,1)}, u32[]{:S(2)}) copy-start(bf16[896,512]{1,0:T(8,128)(2,1)} %get-tuple-element.47.got1) | copy-start | bytes 2752516
  481.4 12.6 %copy-start.4 = (bf16[896,512]{1,0:T(8,128)(2,1)}, bf16[896,512]{1,0:T(8,128)(2,1)S(1)}, u32[]{:S(2)}) copy-start(bf16[896,512]{1,0:T(8,128)(2,1)S(1)} %collective-permute-done.2.got0) | copy-start | bytes 2752516
  481.4 9.6 %collective-permute-start.3 = (bf16[896,512]{1,0:T(8,128)(2,1)S(1)}, bf16[896,512]{1,0:T(8,128)(2,1)S(1)}, u32[]{:S(2)}, u32[]{:S(2)}) collective-permute-start(bf16[896,512]{1,0:T(8,128)(2,1)S(1)} %copy-done.3), channel_id=1, source_target_pairs={{2,0},{14,12},{3,1},{15,13},{18,16},{30,28},{19,17},{31,29}} | collective-permute-start | bytes 2752520 | tf_op jit(solution)/shard_map/ppermute | solution.py:856
  482.7 10.3 %collective-permute-start.4 = (bf16[896,512]{1,0:T(8,128)(2,1)S(1)}, bf16[896,512]{1,0:T(8,128)(2,1)S(1)}, u32[]{:S(2)}, u32[]{:S(2)}) collective-permute-start(bf16[896,512]{1,0:T(8,128)(2,1)S(1)} %collective-permute-done.2.got0), channel_id=1, source_target_pairs={{0,2},{12,14},{1,3},{13,15},{16,18},{28,30},{17,19},{29,31}} | collective-permute-start | bytes 2752520 | tf_op jit(solution)/shard_map/ppermute | solution.py:856
  491.0 2.0 copy-start.5
  493.0 1.0 copy-start.6
  505.2 5.7 copy-start
  505.2 5.7 collective-permute-start.5
  507.1 28.3 %copy-start.7 = (f32[2,8,1,448]{3,2,1,0:T(1,128)S(1)}, f32[2,8,1,448]{3,2,1,0:T(1,128)}, u32[]{:S(2)}) copy-start(f32[2,8,1,448]{3,2,1,0:T(1,128)} %get-tuple-element.58) | copy-start | bytes 86020
  507.1 29.1 %copy-start.8 = (f32[1,3584]{1,0:T(1,128)S(1)}, f32[1,3584]{1,0:T(1,128)}, u32[]{:S(2)}) copy-start(f32[1,3584]{1,0:T(1,128)} %get-tuple-element.55) | copy-start | bytes 43012
  507.1 25.1 %collective-permute-start = (bf16[896,512]{1,0:T(8,128)(2,1)}, bf16[896,512]{1,0:T(8,128)(2,1)}, u32[]{:S(2)}, u32[]{:S(2)}) collective-permute-start(bf16[896,512]{1,0:T(8,128)(2,1)} %get-tuple-element.37), channel_id=1, source_target_pairs={{4,0},{6,2},{8,12},{10,14},{5,1},{7,3},{9,13},{11,15},{20,16},{22,... | collective-permute-start | bytes 2752520 | tf_op jit(solution)/shard_map/ppermute | solution.py:856
  510.9 1.3 copy-start.1
  532.2 4.6 collective-permute-start.7
  534.1 22.4 %collective-permute-start.6 = (bf16[784,512]{1,0:T(8,128)(2,1)}, bf16[784,512]{1,0:T(8,128)(2,1)S(1)}, u32[]{:S(2)}, u32[]{:S(2)}) collective-permute-start(bf16[784,512]{1,0:T(8,128)(2,1)} %get-tuple-element.52), channel_id=1, source_target_pairs={{4,0},{6,2},{8,12},{10,14},{5,1},{7,3},{9,13},{11,15},{20,16},{22,... | collective-permute-start | bytes 2408456 | tf_op jit(solution)/shard_map/ppermute | solution.py:856
  536.9 1.0 copy-start.2
  537.8 20.6 %copy-start.9 = (bf16[112,512]{1,0:T(8,128)(2,1)S(1)}, bf16[112,512]{1,0:T(8,128)(2,1)}, u32[]{:S(2)}) copy-start(bf16[112,512]{1,0:T(8,128)(2,1)} %get-tuple-element.62) | copy-start | bytes 344068
  556.5 12.6 %collective-permute-start.9 = (bf16[784,512]{1,0:T(8,128)(2,1)S(1)}, bf16[784,512]{1,0:T(8,128)(2,1)S(1)}, u32[]{:S(2)}, u32[]{:S(2)}) collective-permute-start(bf16[784,512]{1,0:T(8,128)(2,1)S(1)} %collective-permute-done.6.refs_0_), channel_id=1, source_target_pairs={{0,2},{2,0},{12,14},{14,12},{1,3},{3,1},{13,15},{15,13},{16,18},{1... | collective-permute-start | bytes 2408456 | tf_op jit(solution)/shard_map/ppermute | solution.py:856
  558.5 7.4 %collective-permute-start.8 = (bf16[112,512]{1,0:T(8,128)(2,1)S(1)}, bf16[112,512]{1,0:T(8,128)(2,1)S(1)}, u32[]{:S(2)}, u32[]{:S(2)}) collective-permute-start(bf16[112,512]{1,0:T(8,128)(2,1)S(1)} %copy-done.9), channel_id=1, source_target_pairs={{4,0},{6,2},{8,12},{10,14},{5,1},{7,3},{9,13},{11,15},{20,16},{22,... | collective-permute-start | bytes 344072 | tf_op jit(solution)/shard_map/ppermute | solution.py:856
  565.9 3.2 collective-permute-start.10

commit v5 on v4

--- a/solution.py
+++ b/solution.py
@@ -48,6 +48,7 @@
     steps,
     norms,
     scales,
+    pairs,
     peaks,
     head,
     narrow_head,
@@ -56,6 +57,8 @@
     out_sem,
     scale_sem,
     far_sem,
+    pair_send,
+    pair_recv,
     peak_send,
     peak_recv,
     norm_send,
@@ -136,17 +139,40 @@
         row = jnp.broadcast_to(mix_row[i : i + 1], (LANES, LANES))
         mix[i * LANES : (i + 1) * LANES] = row.T
 
-    def send_peaks(k):
-        @pl.loop(1, ranks)
+    peaks[1:, chips:] = jnp.zeros((parts + 1, ranks - chips, 1, span), jnp.float32)
+
+    def send_peaks(k, mine, stride):
+        @pl.loop(1, ranks // stride)
         def _(step):
             pltpu.make_async_remote_copy(
-                src_ref=peaks.at[k, me],
-                dst_ref=peaks.at[k, me],
+                src_ref=peaks.at[k, mine],
+                dst_ref=peaks.at[k, mine],
                 send_sem=peak_send.at[k],
                 recv_sem=peak_recv.at[k],
-                device_id={"rows": lax.rem(me + step, ranks)},
+                device_id={"rows": lax.rem(me + stride * step, ranks)},
                 device_id_type=MESH,
             ).start()
+
+    def wait_peaks(k, sem):
+        def wait(count):
+            everyone = peaks.at[k, pl.ds(0, count)]
+            pltpu.make_async_copy(everyone, everyone, sem.at[k]).wait()
+
+        if is_static(k):
+            wait(chips - 1 if k else ranks - 1)
+            return
+        pl.when(k == 0)(lambda: wait(ranks - 1))
+        pl.when(k > 0)(lambda: wait(chips - 1))
+
+    def pair(k):
+        return pltpu.make_async_remote_copy(
+            src_ref=pairs.at[k, core],
+            dst_ref=pairs.at[k, core],
+            send_sem=pair_send.at[k],
+            recv_sem=pair_recv.at[k],
+            device_id={"rows": partner},
+            device_id_type=MESH,
+        )
 
     def mixed(k):
         for copy in loads(k):
@@ -174,7 +200,7 @@
             return jnp.maximum(top, jnp.max(jnp.abs(whole).reshape(-1, 8, span), axis=0))
 
         top = lax.fori_loop(0, depth // block, step, jnp.zeros((8, span), jnp.float32))
-        peaks[k, me] = jnp.max(top, axis=0, keepdims=True)
+        return jnp.max(top, axis=0, keepdims=True)
 
     def is_tail(k):
         return is_static(k) and k >= parts
@@ -250,8 +276,7 @@
         return pltpu.make_async_copy(scales.at[k], target, scale_sem.at[k])
 
     def scaled(k):
-        everyone = peaks.at[k, pl.ds(0, ranks - 1)]
-        pltpu.make_async_copy(everyone, everyone, peak_recv.at[k]).wait()
+        wait_peaks(k, peak_recv)
         scale = jnp.max(peaks[k], axis=0)
         scales[k] = scale
 
@@ -274,10 +299,11 @@
         keep(k).start()
         keep_scale(k).start()
 
-    lag = min(3, parts)
-    pl.loop(0, 1)(mixed)
+    lag = min(4, parts)
+    zero = jnp.int32(0)
+    peaks[0, me] = mixed(zero)
     pl.semaphore_wait(barrier, ranks + widths - 2)
-    pl.loop(0, 1)(send_peaks)
+    send_peaks(0, me, 1)
 
     def send_head(to):
         return pltpu.make_async_remote_copy(
@@ -297,11 +323,22 @@
     def _():
         send_head(jnp.where(chip == 1, me - CORES, me + CORES)).start()
 
+    def local(k):
+        pairs[k, core] = mixed(k)
+        pair(k).start()
+
+    def cross(k):
+        pair(k).wait_recv()
+        peaks[k, chip] = jnp.max(pairs[k], axis=0)
+        send_peaks(k, chip, CORES)
+
     def advance(k):
-        mixed(k)
-        send_peaks(k)
-
-    pl.loop(1, lag)(advance)
+        local(k)
+        cross(k)
+
+    pl.loop(1, lag)(local)
+    pl.loop(1, lag)(cross)
+    scaled(zero)
 
     def head_slot():
         return slot(jnp.int32(0), near_rank).at[pl.ds(0, taken)]
@@ -309,26 +346,26 @@
     def keep_head():
         return pltpu.make_async_copy(narrow_head, head_slot(), head_out)
 
-    @pl.loop(0, parts - lag)
+    @pl.when(at_end)
+    def _():
+        send_head(near_rank).wait_recv()
+        narrow_head[...] = (head[...] / scales[0]).astype(jnp.bfloat16)
+        keep_head().start()
+        hop = jnp.where(chip == 0, 1, -1)
+        index = hop + chips - 1
+        pltpu.make_async_remote_copy(
+            src_ref=narrow_head,
+            dst_ref=head_slot(),
+            send_sem=side_send.at[index, 0],
+            recv_sem=side_recv.at[index, 0],
+            device_id={"rows": partner},
+            device_id_type=MESH,
+        ).start()
+
+    @pl.loop(lag, parts)
     def _(k):
-        scaled(k)
-        advance(k + lag)
-
-        @pl.when(at_end & (k == 0))
-        def _():
-            send_head(near_rank).wait_recv()
-            narrow_head[...] = (head[...] / scales[0]).astype(jnp.bfloat16)
-            keep_head().start()
-            hop = jnp.where(chip == 0, 1, -1)
-            index = hop + chips - 1
-            pltpu.make_async_remote_copy(
-                src_ref=narrow_head,
-                dst_ref=head_slot(),
-                send_sem=side_send.at[index, 0],
-                recv_sem=side_recv.at[index, 0],
-                device_id={"rows": partner},
-                device_id_type=MESH,
-            ).start()
+        advance(k)
+        scaled(k - lag + 1)
 
     advance(parts)
     advance(parts + 1)
@@ -344,7 +381,7 @@
             device_id_type=MESH,
         ).start()
 
-    pl.loop(parts - lag, parts)(scaled)
+    pl.loop(parts - lag + 1, parts)(scaled)
     scaled(parts)
     scaled(parts + 1)
 
@@ -475,8 +512,8 @@
                 from_side(k, origin - chip).wait_recv()
 
     def settle(k):
-        everyone = peaks.at[k, pl.ds(0, ranks - 1)]
-        pltpu.make_async_copy(everyone, everyone, peak_send.at[k]).wait()
+        wait_peaks(k, peak_send)
+        pl.when(k > 0)(lambda: pair(k).wait_send())
 
     for k in (last, *late_parts):
         finish(k)
@@ -770,7 +807,7 @@
     chips = ranks // CORES
     bit = norm_train.shape[0]
     late = LATE * span
-    tail = max(8, depth // 64 * 8)
+    tail = max(8, depth // 32 * 8)
     head = min(HEAD, depth // 16 * 8)
     tall = -(-depth // LANES) * LANES
     if tall != depth:
@@ -809,6 +846,7 @@
             pltpu.VMEM((2, 1, bit), jnp.float32),
             pltpu.VMEM((widths, ranks, 1, bit), jnp.float32),
             pltpu.VMEM((parts + 2, 1, span), jnp.float32),
+            pltpu.VMEM((parts + 2, CORES, 1, span), jnp.float32),
             pltpu.VMEM((parts + 2, ranks, 1, span), jnp.float32),
             pltpu.VMEM((head, span), jnp.float32),
             pltpu.VMEM((head, span), jnp.bfloat16),
@@ -817,6 +855,8 @@
             dma((parts + 2,)),
             dma((parts + 2,)),
             dma((LATE + 4,)),
+            dma((parts + 2,)),
+            dma((parts + 2,)),
             dma((parts + 2,)),
             dma((parts + 2,)),
             dma,

time: 571 us -> 571 us (level)
  no operation moved by 1% of the time
where the time goes in v5:
time: 571 us; the launch traced here: 570 us
  Pallas kernels  503 us (88%)
  waiting for transfers between devices  37.5 us (7%)
  starting transfers between devices  23.9 us (4%)
    pallas_call x1, Pallas kernels, shards(): pl.pallas_call(functools.partial(merge, ranks, widths), out_shape=(shape(...  449 us
    ppermute x11, waiting for transfers between devices, send(): lax.ppermute(piece, 'rows', [(source * CORES + a, target * CORES + b) for...  37.5 us
    pallas_call x1, Pallas kernels, settled(): pl.pallas_call(settle_kernel, out_shape=(jax.ShapeDtypeStruct(query.shape...  28.4 us
    pallas_call x3, Pallas kernels, blended(): pl.pallas_call(functools.partial(blend_kernel, ranks, first), out_shape=j...  24.2 us
    ppermute x11, starting transfers between devices, send(): lax.ppermute(piece, 'rows', [(source * CORES + a, target * CORES + b) for...  23.9 us
  transfers between devices with their start and end apart: 11, of which 7 were waited for; matrix products, arithmetic and copies ran while one was open for 0% of the time, Pallas kernels for 9%

profile of v5, /device:TPU:0, one launch (start us, length us, event | category | flops | bytes accessed | tf_op | source)
XLA Modules:
  0.0 569.7 jit_solution(9127445342075158505)
XLA Ops:
  0.6 448.9 %shard_map.144 = (bf16[7168,3584]{1,0:T(8,128)(2,1)}, bf16[7168,512]{1,0:T(8,128)(2,1)}, bf16[7168,512]{1,0:T(8,128)(2,1)}, bf16[896,512]{1,0:T(8,128)(2,1)}, bf...) custom-call(f32[896,3584]{1,0:T(8,128)} %one_query.1, ...), custom_call_target="tpu_custom_call" | custom-call | tf_op jit(solution)/shard_map/pallas_call | solution.py:822
  449.6 1.3 collective-permute-start.2
  450.9 1.3 collective-permute-start.1
  452.2 0.0 copy-start.3
  452.2 28.4 %shard_map.145 = (bf16[7168,3584]{1,0:T(8,128)(2,1)}, bf16[7168,512]{1,0:T(8,128)(2,1)}, f32[1,512]{1,0:T(1,128)}, f32[1,512]{1,0:T(1,128)}, f32[8,128]{1,0:T(8,128)}) custom-call(bf16[7168,3584]{1,0:T(8,128)(2,1)} %get-tuple-element.39.query.whole, bf16[7168,512]{1,0:T(8,128)(2,1)} %get-tuple-element.40.value, f32[1,512]{1,0:T(1,128)} %get-tuple-element.41.scale_key, ...), custom_call_target="tpu_custom_call" | custom-call | bytes 73400320 | tf_op jit(solution)/shard_map/pallas_call | solution.py:666
  480.6 0.0 collective-permute-done.2.got0
  480.6 0.0 copy-start.4
  480.6 0.0 copy-done.3
  480.6 1.3 collective-permute-start.3
  481.9 8.4 %collective-permute-start.4 = (bf16[896,512]{1,0:T(8,128)(2,1)S(1)}, bf16[896,512]{1,0:T(8,128)(2,1)S(1)}, u32[]{:S(2)}, u32[]{:S(2)}) collective-permute-start(bf16[896,512]{1,0:T(8,128)(2,1)S(1)} %collective-permute-done.2.got0), channel_id=1, source_target_pairs={{0,2},{12,14},{1,3},{13,15},{16,18},{28,30},{17,19},{29,31}} | collective-permute-start | bytes 2752520 | tf_op jit(solution)/shard_map/ppermute | solution.py:896
  490.4 0.0 collective-permute-done.3.side0
  490.4 0.0 copy-start.5
  490.4 2.0 collective-permute-done.4.side1
  492.4 0.0 copy-done.5
  492.4 0.0 copy-start.6
  492.4 1.0 copy-done.6
  493.4 0.0 copy-done.4
  493.4 6.7 %shard_map.146.fresh = bf16[7168,3584]{1,0:T(8,128)(2,1)} custom-call(bf16[7168,3584]{1,0:T(8,128)(2,1)} %get-tuple-element.43.fresh, bf16[7168,3584]{1,0:T(8,128)(2,1)} %get-tuple-element.39.query.whole, bf16[896,512]{1,0:T(8,128)(2,1)} %copy-done.4, bf16[896,512]{1,0:T(8,128)(2,1)} %get-tuple-element.47.got1, ...), custom_call_target="tpu_custom_call", output_to_operand_aliasing={{}: (0, {})} | custom-call | bytes 14680064 | tf_op jit(solution)/shard_map/pallas_call | solution.py:736
  500.1 4.3 collective-permute-done.1.got0.got1
  504.4 0.0 copy-start
  504.4 1.9 collective-permute-start.5
  506.3 0.0 copy-start.7
  506.3 0.0 copy-start.8
  506.3 1.4 collective-permute-start
  507.8 2.3 collective-permute-done.5.side0.side1
  510.1 0.0 copy-done
  510.1 0.0 copy-start.1
  510.1 1.3 copy-done.1
  511.3 10.8 %shard_map.147 = bf16[7168,3584]{1,0:T(8,128)(2,1)} custom-call(bf16[7168,3584]{1,0:T(8,128)(2,1)} %shard_map.146.fresh, bf16[7168,3584]{1,0:T(8,128)(2,1)} %get-tuple-element.39.query.whole, bf16[896,1024]{1,0:T(8,128)(2,1)} %copy-done, bf16[896,1024]{1,0:T(8,128)(2,1)} %copy-done, bf16[896,1024]{1,0:T(8,128)(2,1)} %copy-done.1, ...), custom_call_target="tpu_custom_call", output_to_operand_aliasing={{}: (0, {})} | custom-call | bytes 29360128 | tf_op jit(solution)/shard_map/pallas_call | solution.py:736
  522.1 9.3 %collective-permute-done.got0.got1 = bf16[896,512]{1,0:T(8,128)(2,1)} collective-permute-done((bf16[896,512]{1,0:T(8,128)(2,1)}, bf16[896,512]{1,0:T(8,128)(2,1)}, u32[]{:S(2)}, u32[]{:S(2)}) %collective-permute-start) | collective-permute-done | bytes 917536 | tf_op jit(solution)/shard_map/ppermute | solution.py:896
  531.4 1.9 collective-permute-start.7
  533.3 1.3 collective-permute-start.6
  534.6 0.0 copy-done.7
  534.7 0.7 convert_element_type.11
  535.4 0.0 copy-done.8
  535.4 0.6 reduce
  536.1 0.0 collective-permute-done.7.side0.side1
  536.1 0.0 copy-start.2
  536.1 0.9 copy-done.2
  537.0 0.0 copy-start.9
  537.0 6.7 %shard_map.148 = bf16[7168,512]{1,0:T(8,128)(2,1)} custom-call(f32[8,128]{1,0:T(8,128)} %get-tuple-element.48.done.fresh, bf16[7168,512]{1,0:T(8,128)(2,1)} %get-tuple-element.53.whole, bf16[896,512]{1,0:T(8,128)(2,1)} %collective-permute-done.got0.got1, bf16[896,512]{1,0:T(8,128)(2,1)} %collective-permute-done.got0.got1, bf16[896,512]{1,0:T(8,128)(2,1)} %copy-done.2, ...), custom_call_target="tpu_custom_call" | custom-call | bytes 14680064 | tf_op jit(solution)/shard_map/pallas_call | solution.py:736
  543.7 9.6 %collective-permute-done.6.refs_0_ = bf16[672,512]{1,0:T(8,128)(2,1)S(1)} collective-permute-done((bf16[672,512]{1,0:T(8,128)(2,1)}, bf16[672,512]{1,0:T(8,128)(2,1)S(1)}, u32[]{:S(2)}, u32[]{:S(2)}) %collective-permute-start.6) | collective-permute-done | bytes 688160 | tf_op jit(solution)/shard_map/ppermute | solution.py:896
  553.3 1.9 collective-permute-start.9
  555.2 0.0 copy-done.9
  555.2 1.3 collective-permute-start.8
  556.5 8.6 %collective-permute-done.8.refs_1_ = bf16[224,512]{1,0:T(8,128)(2,1)S(1)} collective-permute-done((bf16[224,512]{1,0:T(8,128)(2,1)S(1)}, bf16[224,512]{1,0:T(8,128)(2,1)S(1)}, u32[]{:S(2)}, u32[]{:S(2)}) %collective-permute-start.8) | collective-permute-done | bytes 229408 | tf_op jit(solution)/shard_map/ppermute | solution.py:896
  565.1 1.9 collective-permute-start.10
  567.0 1.5 collective-permute-done.10.refs_3_
  568.5 0.0 collective-permute-done.9.refs_2_
  568.5 1.3 shard_map.149
  (2 shorter events, 0.1 us)
Async XLA Ops:
  449.6 31.0 %collective-permute-start.2 = (bf16[896,512]{1,0:T(8,128)(2,1)}, bf16[896,512]{1,0:T(8,128)(2,1)S(1)}, u32[]{:S(2)}, u32[]{:S(2)}) collective-permute-start(bf16[896,512]{1,0:T(8,128)(2,1)} %get-tuple-element.47.got1), channel_id=1, source_target_pairs={{4,0},{8,12},{5,1},{9,13},{20,16},{24,28},{21,17},{25,29}} | collective-permute-start | bytes 2752520 | tf_op jit(solution)/shard_map/ppermute | solution.py:896
  450.9 53.5 %collective-permute-start.1 = (bf16[896,1024]{1,0:T(8,128)(2,1)}, bf16[896,1024]{1,0:T(8,128)(2,1)S(1)}, u32[]{:S(2)}, u32[]{:S(2)}) collective-permute-start(bf16[896,1024]{1,0:T(8,128)(2,1)} %get-tuple-element.38), channel_id=1, source_target_pairs={{4,0},{6,2},{8,12},{10,14},{5,1},{7,3},{9,13},{11,15},{20,16},{22,... | collective-permute-start | bytes 5505032 | tf_op jit(solution)/shard_map/ppermute | solution.py:896
  452.2 28.5 %copy-start.3 = (bf16[896,512]{1,0:T(8,128)(2,1)S(1)}, bf16[896,512]{1,0:T(8,128)(2,1)}, u32[]{:S(2)}) copy-start(bf16[896,512]{1,0:T(8,128)(2,1)} %get-tuple-element.47.got1) | copy-start | bytes 2752516
  480.6 12.8 %copy-start.4 = (bf16[896,512]{1,0:T(8,128)(2,1)}, bf16[896,512]{1,0:T(8,128)(2,1)S(1)}, u32[]{:S(2)}) copy-start(bf16[896,512]{1,0:T(8,128)(2,1)S(1)} %collective-permute-done.2.got0) | copy-start | bytes 2752516
  480.6 9.7 %collective-permute-start.3 = (bf16[896,512]{1,0:T(8,128)(2,1)S(1)}, bf16[896,512]{1,0:T(8,128)(2,1)S(1)}, u32[]{:S(2)}, u32[]{:S(2)}) collective-permute-start(bf16[896,512]{1,0:T(8,128)(2,1)S(1)} %copy-done.3), channel_id=1, source_target_pairs={{2,0},{14,12},{3,1},{15,13},{18,16},{30,28},{19,17},{31,29}} | collective-permute-start | bytes 2752520 | tf_op jit(solution)/shard_map/ppermute | solution.py:896
  481.9 10.5 %collective-permute-start.4 = (bf16[896,512]{1,0:T(8,128)(2,1)S(1)}, bf16[896,512]{1,0:T(8,128)(2,1)S(1)}, u32[]{:S(2)}, u32[]{:S(2)}) collective-permute-start(bf16[896,512]{1,0:T(8,128)(2,1)S(1)} %collective-permute-done.2.got0), channel_id=1, source_target_pairs={{0,2},{12,14},{1,3},{13,15},{16,18},{28,30},{17,19},{29,31}} | collective-permute-start | bytes 2752520 | tf_op jit(solution)/shard_map/ppermute | solution.py:896
  490.4 2.0 copy-start.5
  492.4 1.0 copy-start.6
  504.4 5.7 copy-start
  504.4 5.7 collective-permute-start.5
  506.3 28.3 %copy-start.7 = (f32[2,8,1,448]{3,2,1,0:T(1,128)S(1)}, f32[2,8,1,448]{3,2,1,0:T(1,128)}, u32[]{:S(2)}) copy-start(f32[2,8,1,448]{3,2,1,0:T(1,128)} %get-tuple-element.58) | copy-start | bytes 86020
  506.3 29.1 %copy-start.8 = (f32[1,3584]{1,0:T(1,128)S(1)}, f32[1,3584]{1,0:T(1,128)}, u32[]{:S(2)}) copy-start(f32[1,3584]{1,0:T(1,128)} %get-tuple-element.55) | copy-start | bytes 43012
  506.3 25.1 %collective-permute-start = (bf16[896,512]{1,0:T(8,128)(2,1)}, bf16[896,512]{1,0:T(8,128)(2,1)}, u32[]{:S(2)}, u32[]{:S(2)}) collective-permute-start(bf16[896,512]{1,0:T(8,128)(2,1)} %get-tuple-element.37), channel_id=1, source_target_pairs={{4,0},{6,2},{8,12},{10,14},{5,1},{7,3},{9,13},{11,15},{20,16},{22,... | collective-permute-start | bytes 2752520 | tf_op jit(solution)/shard_map/ppermute | solution.py:896
  510.1 1.3 copy-start.1
  531.4 4.6 collective-permute-start.7
  533.3 19.9 %collective-permute-start.6 = (bf16[672,512]{1,0:T(8,128)(2,1)}, bf16[672,512]{1,0:T(8,128)(2,1)S(1)}, u32[]{:S(2)}, u32[]{:S(2)}) collective-permute-start(bf16[672,512]{1,0:T(8,128)(2,1)} %get-tuple-element.52), channel_id=1, source_target_pairs={{4,0},{6,2},{8,12},{10,14},{5,1},{7,3},{9,13},{11,15},{20,16},{22,... | collective-permute-start | bytes 2064392 | tf_op jit(solution)/shard_map/ppermute | solution.py:896
  536.1 1.0 copy-start.2
  537.0 18.2 %copy-start.9 = (bf16[224,512]{1,0:T(8,128)(2,1)S(1)}, bf16[224,512]{1,0:T(8,128)(2,1)}, u32[]{:S(2)}) copy-start(bf16[224,512]{1,0:T(8,128)(2,1)} %get-tuple-element.62) | copy-start | bytes 688132
  553.3 15.2 %collective-permute-start.9 = (bf16[672,512]{1,0:T(8,128)(2,1)S(1)}, bf16[672,512]{1,0:T(8,128)(2,1)S(1)}, u32[]{:S(2)}, u32[]{:S(2)}) collective-permute-start(bf16[672,512]{1,0:T(8,128)(2,1)S(1)} %collective-permute-done.6.refs_0_), channel_id=1, source_target_pairs={{0,2},{2,0},{12,14},{14,12},{1,3},{3,1},{13,15},{15,13},{16,18},{1... | collective-permute-start | bytes 2064392 | tf_op jit(solution)/shard_map/ppermute | solution.py:896
  555.2 9.9 %collective-permute-start.8 = (bf16[224,512]{1,0:T(8,128)(2,1)S(1)}, bf16[224,512]{1,0:T(8,128)(2,1)S(1)}, u32[]{:S(2)}, u32[]{:S(2)}) collective-permute-start(bf16[224,512]{1,0:T(8,128)(2,1)S(1)} %copy-done.9), channel_id=1, source_target_pairs={{4,0},{6,2},{8,12},{10,14},{5,1},{7,3},{9,13},{11,15},{20,16},{22,... | collective-permute-start | bytes 688136 | tf_op jit(solution)/shard_map/ppermute | solution.py:896
  565.1 3.4 collective-permute-start.10

commit v6 on v5

--- a/solution.py
+++ b/solution.py
@@ -750,42 +750,37 @@
     )(fresh, whole, *gots, *sides, done)
 
 
-def place_kernel(ranks, depth, _, *refs):
-    gots, sides, (target, sems) = refs[0:2], refs[2:4], refs[4:]
+def place_kernel(ranks, depth, first, _, got, side, target, sems):
     at_end, straight, crossed = far_ranks(ranks)
 
     @pl.when(at_end)
     def _():
         copies = []
-        for rank, pieces in ((straight, gots), (crossed, sides)):
-            row = rank * depth
-            for piece in pieces:
-                rows = pl.ds(pl.multiple_of(row, 8), piece.shape[0])
-                at = sems.at[len(copies)]
-                copies.append(pltpu.make_async_copy(piece, target.at[rows], at))
-                row = row + piece.shape[0]
+        for at, (rank, piece) in enumerate(((straight, got), (crossed, side))):
+            rows = pl.ds(pl.multiple_of(rank * depth + first, 8), piece.shape[0])
+            copies.append(pltpu.make_async_copy(piece, target.at[rows], sems.at[at]))
         for copy in copies:
             copy.start()
         for copy in copies:
             copy.wait()
 
 
-def placed(ranks, whole, gots, sides):
+def placed(ranks, first, whole, got, side):
     anywhere = pl.BlockSpec(memory_space=pl.ANY)
     near = pl.BlockSpec(memory_space=pltpu.VMEM)
     depth = whole.shape[0] // ranks
     return pl.pallas_call(
-        functools.partial(place_kernel, ranks, depth),
+        functools.partial(place_kernel, ranks, depth, first),
         out_shape=jax.ShapeDtypeStruct(whole.shape, whole.dtype),
-        in_specs=[anywhere, near, near, near, near],
+        in_specs=[anywhere, near, near],
         out_specs=anywhere,
-        scratch_shapes=[pltpu.SemaphoreType.DMA((4,))],
+        scratch_shapes=[pltpu.SemaphoreType.DMA((2,))],
         input_output_aliases={0: 0},
         compiler_params=pltpu.CompilerParams(vmem_limit_bytes=8 * 2**20),
         cost_estimate=pl.CostEstimate(
-            flops=0, bytes_accessed=8 * gots[0].size, transcendentals=0
+            flops=0, bytes_accessed=8 * got.size, transcendentals=0
         ),
-    )(whole, *gots, *sides)
+    )(whole, got, side)
 
 
 def shards(
@@ -938,8 +933,10 @@
     got_key, new_query = lax.optimization_barrier((got_key, new_query))
     new_key = blended(ranks, 0, done, key, [got_key] * 2, [to_side(got_key)] * 2, done)
     got_value, new_key, small = lax.optimization_barrier((got_value, new_key, small))
-    sides = to_side(got_value), to_side(got_rest)
-    new_value = placed(ranks, new_value, (got_value, got_rest), sides)
+    side_value = to_side(got_value)
+    side_rest = to_side(got_rest)
+    new_value = placed(ranks, 0, new_value, got_value, side_value)
+    new_value = placed(ranks, depth - tail, new_value, got_rest, side_rest)
     return (new_query, new_key, new_value, *small)
 
 

time: 571 us -> 570 us (level)
  no operation moved by 1% of the time
where the time goes in v6:
time: 570 us; the launch traced here: 569 us
  Pallas kernels  503 us (88%)
  waiting for transfers between devices  36.4 us (6%)
  starting transfers between devices  23.9 us (4%)
    pallas_call x1, Pallas kernels, shards(): pl.pallas_call(functools.partial(merge, ranks, widths), out_shape=(shape(...  449 us
    ppermute x11, waiting for transfers between devices, send(): lax.ppermute(piece, 'rows', [(source * CORES + a, target * CORES + b) for...  36.4 us
    pallas_call x1, Pallas kernels, settled(): pl.pallas_call(settle_kernel, out_shape=(jax.ShapeDtypeStruct(query.shape...  28.4 us
    pallas_call x3, Pallas kernels, blended(): pl.pallas_call(functools.partial(blend_kernel, ranks, first), out_shape=j...  24.2 us
    ppermute x11, starting transfers between devices, send(): lax.ppermute(piece, 'rows', [(source * CORES + a, target * CORES + b) for...  23.9 us
  transfers between devices with their start and end apart: 11, of which 7 were waited for; matrix products, arithmetic and copies ran while one was open for 0% of the time, Pallas kernels for 9%

profile of v6, /device:TPU:0, one launch (start us, length us, event | category | flops | bytes accessed | tf_op | source)
XLA Modules:
  0.0 569.3 jit_solution(8171066037029594741)
XLA Ops:
  0.6 448.9 %shard_map.144 = (bf16[7168,3584]{1,0:T(8,128)(2,1)}, bf16[7168,512]{1,0:T(8,128)(2,1)}, bf16[7168,512]{1,0:T(8,128)(2,1)}, bf16[896,512]{1,0:T(8,128)(2,1)}, bf...) custom-call(f32[896,3584]{1,0:T(8,128)} %one_query.1, ...), custom_call_target="tpu_custom_call" | custom-call | tf_op jit(solution)/shard_map/pallas_call | solution.py:817
  449.6 1.3 collective-permute-start.2
  450.9 1.3 collective-permute-start.1
  452.2 0.0 copy-start.3
  452.2 28.4 %shard_map.145 = (bf16[7168,3584]{1,0:T(8,128)(2,1)}, bf16[7168,512]{1,0:T(8,128)(2,1)}, f32[1,512]{1,0:T(1,128)}, f32[1,512]{1,0:T(1,128)}, f32[8,128]{1,0:T(8,128)}) custom-call(bf16[7168,3584]{1,0:T(8,128)(2,1)} %get-tuple-element.39.query.whole, bf16[7168,512]{1,0:T(8,128)(2,1)} %get-tuple-element.40.value, f32[1,512]{1,0:T(1,128)} %get-tuple-element.41.scale_key, ...), custom_call_target="tpu_custom_call" | custom-call | bytes 73400320 | tf_op jit(solution)/shard_map/pallas_call | solution.py:666
  480.6 0.0 collective-permute-done.2.got0
  480.6 0.0 copy-start.4
  480.6 0.0 copy-done.3
  480.6 1.3 collective-permute-start.3
  481.9 8.4 %collective-permute-start.4 = (bf16[896,512]{1,0:T(8,128)(2,1)S(1)}, bf16[896,512]{1,0:T(8,128)(2,1)S(1)}, u32[]{:S(2)}, u32[]{:S(2)}) collective-permute-start(bf16[896,512]{1,0:T(8,128)(2,1)S(1)} %collective-permute-done.2.got0), channel_id=1, source_target_pairs={{0,2},{12,14},{1,3},{13,15},{16,18},{28,30},{17,19},{29,31}} | collective-permute-start | bytes 2752520 | tf_op jit(solution)/shard_map/ppermute | solution.py:891
  490.4 0.0 collective-permute-done.3.side0
  490.4 0.0 copy-start.5
  490.4 2.0 collective-permute-done.4.side1
  492.4 0.0 copy-done.5
  492.4 0.0 copy-start.6
  492.4 1.0 copy-done.6
  493.4 0.0 copy-done.4
  493.4 6.7 %shard_map.146.fresh = bf16[7168,3584]{1,0:T(8,128)(2,1)} custom-call(bf16[7168,3584]{1,0:T(8,128)(2,1)} %get-tuple-element.43.fresh, bf16[7168,3584]{1,0:T(8,128)(2,1)} %get-tuple-element.39.query.whole, bf16[896,512]{1,0:T(8,128)(2,1)} %copy-done.4, bf16[896,512]{1,0:T(8,128)(2,1)} %get-tuple-element.47.got1, ...), custom_call_target="tpu_custom_call", output_to_operand_aliasing={{}: (0, {})} | custom-call | bytes 14680064 | tf_op jit(solution)/shard_map/pallas_call | solution.py:736
  500.1 4.3 collective-permute-done.1.got0.got1
  504.4 0.0 copy-start
  504.4 1.9 collective-permute-start.5
  506.3 0.0 copy-start.7
  506.3 0.0 copy-start.8
  506.3 1.4 collective-permute-start
  507.8 2.3 collective-permute-done.5.side0.side1
  510.1 0.0 copy-done
  510.1 0.0 copy-start.1
  510.1 1.3 copy-done.1
  511.3 10.8 %shard_map.147 = bf16[7168,3584]{1,0:T(8,128)(2,1)} custom-call(bf16[7168,3584]{1,0:T(8,128)(2,1)} %shard_map.146.fresh, bf16[7168,3584]{1,0:T(8,128)(2,1)} %get-tuple-element.39.query.whole, bf16[896,1024]{1,0:T(8,128)(2,1)} %copy-done, bf16[896,1024]{1,0:T(8,128)(2,1)} %copy-done, bf16[896,1024]{1,0:T(8,128)(2,1)} %copy-done.1, ...), custom_call_target="tpu_custom_call", output_to_operand_aliasing={{}: (0, {})} | custom-call | bytes 29360128 | tf_op jit(solution)/shard_map/pallas_call | solution.py:736
  522.1 9.3 %collective-permute-done.got0.got1 = bf16[896,512]{1,0:T(8,128)(2,1)} collective-permute-done((bf16[896,512]{1,0:T(8,128)(2,1)}, bf16[896,512]{1,0:T(8,128)(2,1)}, u32[]{:S(2)}, u32[]{:S(2)}) %collective-permute-start) | collective-permute-done | bytes 917536 | tf_op jit(solution)/shard_map/ppermute | solution.py:891
  531.4 1.9 collective-permute-start.7
  533.3 1.3 collective-permute-start.6
  534.6 0.0 copy-done.7
  534.7 0.7 convert_element_type.11
  535.4 0.0 copy-done.8
  535.4 0.6 reduce
  536.1 0.0 collective-permute-done.7.side0.side1
  536.1 0.0 copy-start.2
  536.1 0.9 copy-done.2
  537.0 0.0 copy-start.9
  537.0 6.7 %shard_map.148 = bf16[7168,512]{1,0:T(8,128)(2,1)} custom-call(f32[8,128]{1,0:T(8,128)} %get-tuple-element.48.done.fresh, bf16[7168,512]{1,0:T(8,128)(2,1)} %get-tuple-element.53.whole, bf16[896,512]{1,0:T(8,128)(2,1)} %collective-permute-done.got0.got1, bf16[896,512]{1,0:T(8,128)(2,1)} %collective-permute-done.got0.got1, bf16[896,512]{1,0:T(8,128)(2,1)} %copy-done.2, ...), custom_call_target="tpu_custom_call" | custom-call | bytes 14680064 | tf_op jit(solution)/shard_map/pallas_call | solution.py:736
  543.7 9.6 %collective-permute-done.6.got = bf16[672,512]{1,0:T(8,128)(2,1)S(1)} collective-permute-done((bf16[672,512]{1,0:T(8,128)(2,1)}, bf16[672,512]{1,0:T(8,128)(2,1)S(1)}, u32[]{:S(2)}, u32[]{:S(2)}) %collective-permute-start.6) | collective-permute-done | bytes 688160 | tf_op jit(solution)/shard_map/ppermute | solution.py:891
  553.3 1.9 collective-permute-start.8
  555.2 0.0 copy-done.9
  555.2 1.3 collective-permute-start.9
  556.5 8.6 %collective-permute-done.9.got = bf16[224,512]{1,0:T(8,128)(2,1)S(1)} collective-permute-done((bf16[224,512]{1,0:T(8,128)(2,1)S(1)}, bf16[224,512]{1,0:T(8,128)(2,1)S(1)}, u32[]{:S(2)}, u32[]{:S(2)}) %collective-permute-start.9) | collective-permute-done | bytes 229408 | tf_op jit(solution)/shard_map/ppermute | solution.py:891
  565.1 1.9 collective-permute-start.10
  567.0 0.0 collective-permute-done.8.side
  567.0 1.1 shard_map.149._
  568.2 0.3 collective-permute-done.10.side
  568.5 0.8 shard_map.150
  (2 shorter events, 0.1 us)
Async XLA Ops:
  449.6 31.0 %collective-permute-start.2 = (bf16[896,512]{1,0:T(8,128)(2,1)}, bf16[896,512]{1,0:T(8,128)(2,1)S(1)}, u32[]{:S(2)}, u32[]{:S(2)}) collective-permute-start(bf16[896,512]{1,0:T(8,128)(2,1)} %get-tuple-element.47.got1), channel_id=1, source_target_pairs={{4,0},{8,12},{5,1},{9,13},{20,16},{24,28},{21,17},{25,29}} | collective-permute-start | bytes 2752520 | tf_op jit(solution)/shard_map/ppermute | solution.py:891
  450.9 53.5 %collective-permute-start.1 = (bf16[896,1024]{1,0:T(8,128)(2,1)}, bf16[896,1024]{1,0:T(8,128)(2,1)S(1)}, u32[]{:S(2)}, u32[]{:S(2)}) collective-permute-start(bf16[896,1024]{1,0:T(8,128)(2,1)} %get-tuple-element.38), channel_id=1, source_target_pairs={{4,0},{6,2},{8,12},{10,14},{5,1},{7,3},{9,13},{11,15},{20,16},{22,... | collective-permute-start | bytes 5505032 | tf_op jit(solution)/shard_map/ppermute | solution.py:891
  452.2 28.5 %copy-start.3 = (bf16[896,512]{1,0:T(8,128)(2,1)S(1)}, bf16[896,512]{1,0:T(8,128)(2,1)}, u32[]{:S(2)}) copy-start(bf16[896,512]{1,0:T(8,128)(2,1)} %get-tuple-element.47.got1) | copy-start | bytes 2752516
  480.6 12.8 %copy-start.4 = (bf16[896,512]{1,0:T(8,128)(2,1)}, bf16[896,512]{1,0:T(8,128)(2,1)S(1)}, u32[]{:S(2)}) copy-start(bf16[896,512]{1,0:T(8,128)(2,1)S(1)} %collective-permute-done.2.got0) | copy-start | bytes 2752516
  480.6 9.7 %collective-permute-start.3 = (bf16[896,512]{1,0:T(8,128)(2,1)S(1)}, bf16[896,512]{1,0:T(8,128)(2,1)S(1)}, u32[]{:S(2)}, u32[]{:S(2)}) collective-permute-start(bf16[896,512]{1,0:T(8,128)(2,1)S(1)} %copy-done.3), channel_id=1, source_target_pairs={{2,0},{14,12},{3,1},{15,13},{18,16},{30,28},{19,17},{31,29}} | collective-permute-start | bytes 2752520 | tf_op jit(solution)/shard_map/ppermute | solution.py:891
  481.9 10.5 %collective-permute-start.4 = (bf16[896,512]{1,0:T(8,128)(2,1)S(1)}, bf16[896,512]{1,0:T(8,128)(2,1)S(1)}, u32[]{:S(2)}, u32[]{:S(2)}) collective-permute-start(bf16[896,512]{1,0:T(8,128)(2,1)S(1)} %collective-permute-done.2.got0), channel_id=1, source_target_pairs={{0,2},{12,14},{1,3},{13,15},{16,18},{28,30},{17,19},{29,31}} | collective-permute-start | bytes 2752520 | tf_op jit(solution)/shard_map/ppermute | solution.py:891
  490.4 2.0 copy-start.5
  492.4 1.0 copy-start.6
  504.4 5.7 copy-start
  504.4 5.7 collective-permute-start.5
  506.3 28.3 %copy-start.7 = (f32[2,8,1,448]{3,2,1,0:T(1,128)S(1)}, f32[2,8,1,448]{3,2,1,0:T(1,128)}, u32[]{:S(2)}) copy-start(f32[2,8,1,448]{3,2,1,0:T(1,128)} %get-tuple-element.58) | copy-start | bytes 86020
  506.3 29.1 %copy-start.8 = (f32[1,3584]{1,0:T(1,128)S(1)}, f32[1,3584]{1,0:T(1,128)}, u32[]{:S(2)}) copy-start(f32[1,3584]{1,0:T(1,128)} %get-tuple-element.55) | copy-start | bytes 43012
  506.3 25.1 %collective-permute-start = (bf16[896,512]{1,0:T(8,128)(2,1)}, bf16[896,512]{1,0:T(8,128)(2,1)}, u32[]{:S(2)}, u32[]{:S(2)}) collective-permute-start(bf16[896,512]{1,0:T(8,128)(2,1)} %get-tuple-element.37), channel_id=1, source_target_pairs={{4,0},{6,2},{8,12},{10,14},{5,1},{7,3},{9,13},{11,15},{20,16},{22,... | collective-permute-start | bytes 2752520 | tf_op jit(solution)/shard_map/ppermute | solution.py:891
  510.1 1.3 copy-start.1
  531.4 4.6 collective-permute-start.7
  533.3 19.9 %collective-permute-start.6 = (bf16[672,512]{1,0:T(8,128)(2,1)}, bf16[672,512]{1,0:T(8,128)(2,1)S(1)}, u32[]{:S(2)}, u32[]{:S(2)}) collective-permute-start(bf16[672,512]{1,0:T(8,128)(2,1)} %get-tuple-element.52), channel_id=1, source_target_pairs={{4,0},{6,2},{8,12},{10,14},{5,1},{7,3},{9,13},{11,15},{20,16},{22,... | collective-permute-start | bytes 2064392 | tf_op jit(solution)/shard_map/ppermute | solution.py:891
  536.1 1.0 copy-start.2
  537.0 18.2 %copy-start.9 = (bf16[224,512]{1,0:T(8,128)(2,1)S(1)}, bf16[224,512]{1,0:T(8,128)(2,1)}, u32[]{:S(2)}) copy-start(bf16[224,512]{1,0:T(8,128)(2,1)} %get-tuple-element.62) | copy-start | bytes 688132
  553.3 13.7 %collective-permute-start.8 = (bf16[672,512]{1,0:T(8,128)(2,1)S(1)}, bf16[672,512]{1,0:T(8,128)(2,1)S(1)}, u32[]{:S(2)}, u32[]{:S(2)}) collective-permute-start(bf16[672,512]{1,0:T(8,128)(2,1)S(1)} %collective-permute-done.6.got), channel_id=1, source_target_pairs={{0,2},{2,0},{12,14},{14,12},{1,3},{3,1},{13,15},{15,13},{16,18},{1... | collective-permute-start | bytes 2064392 | tf_op jit(solution)/shard_map/ppermute | solution.py:891
  555.2 9.9 %collective-permute-start.9 = (bf16[224,512]{1,0:T(8,128)(2,1)S(1)}, bf16[224,512]{1,0:T(8,128)(2,1)S(1)}, u32[]{:S(2)}, u32[]{:S(2)}) collective-permute-start(bf16[224,512]{1,0:T(8,128)(2,1)S(1)} %copy-done.9), channel_id=1, source_target_pairs={{4,0},{6,2},{8,12},{10,14},{5,1},{7,3},{9,13},{11,15},{20,16},{22,... | collective-permute-start | bytes 688136 | tf_op jit(solution)/shard_map/ppermute | solution.py:891
  565.1 3.4 collective-permute-start.10
